TPU v7x, 128 devices: a whole 4x4x4 slice. The times are simulated.
128 devices in a mesh: img: 16 (over z, y_hi, core), feat: 8 (over y_lo, x).
Axes of the slice: x: 4, y: 4 (y_hi: 2, y_lo: 2; y = y_hi * 2 + y_lo), z: 4, core: 2. Of those that a mesh axis runs over, the one named last changes fastest.
Arguments:
- features: bfloat16 [16384, 32768], P('img', 'feat'), may hold values from -0.055242717 to 0.055242717
- weights: bfloat16 [512, 32768], P('img', 'feat'), may hold values from -20 to 20
- direction: bfloat16 [512, 32768], P('img', 'feat'), may hold values from -6 to 6
Outputs:
- hessian_product: float32 [512, 32768], P('img', 'feat')
All inputs are finite; a program needn't handle non-finite values.
Results may differ from a plain program's by a relative error of at most 0.0024.
Values may be sent and summed in bfloat16 or wider, within the bound.
A program may use at most 64 MiB of HBM per device.

v0:
```python
import jax
import jax.numpy as jnp
from jax import lax
from jax.sharding import PartitionSpec as P


def in_order(parts, dim):
    shape = list(parts.shape[1:])
    shape[dim] *= parts.shape[0]
    return jnp.moveaxis(parts, 0, dim).reshape(shape)


def from_everyone(shard, axis):
    length = lax.axis_size(axis)
    return lax.all_to_all(
        jnp.broadcast_to(shard[None], (length, *shard.shape)), axis, 0, 0, tiled=True
    )


def gathered_copies(shard, axis, dim):
    return in_order(from_everyone(shard, axis), dim)


def weigh(pair):
    prob = jax.nn.sigmoid(pair[0])
    return (prob * (1.0 - prob) * pair[1]).astype(jnp.bfloat16)


def body(features, weights, direction):
    stacked = jnp.stack((weights, direction))
    partial_scores = jnp.einsum(
        "rf,kcf->krc",
        features,
        lax.all_gather(stacked, "img", axis=1, tiled=True),
        preferred_element_type=jnp.float32,
    )
    shares = lax.psum_scatter(partial_scores, "feat", scatter_dimension=1, tiled=True)
    curvature = gathered_copies(weigh(shares), "feat", 0)
    summed_terms = lax.psum_scatter(
        lax.dot_general(
            curvature, features, (((0,), (0,)), ((), ())), preferred_element_type=jnp.float32
        ),
        "img",
        scatter_dimension=0,
        tiled=True,
    )
    return 4.0 * summed_terms


def solution(mesh):
    placed = (P("img", "feat"), P("img", "feat"), P("img", "feat"))
    return jax.shard_map(
        body, mesh=mesh, in_specs=placed, out_specs=P("img", "feat"), check_vma=False
    )
```

profile of v0, /device:TPU:0, one launch (start us, length us, event | category | flops | bytes accessed | tf_op | source)
XLA Modules:
  0.0 291.0 jit_solution(6749987864184155752)
XLA Ops:
  6.5 0.0 all-gather.2.cloned.1.call-start
  6.5 1.9 pad_maximum_fusion
  8.4 0.0 all-gather.2.cloned.1.call-update
  8.4 0.0 reduce-scatter.3.cloned.1.call-start
  8.5 76.7 %all-gather.2.cloned.1.call-done = bf16[2,512,4096]{2,1,0:T(8,128)(2,1)} async-done(((bf16[2,32,4096]{2,1,0:T(8,128)(2,1)}), bf16[2,512,4096]{2,1,0:T(8,128)(2,1)}) %all-gather.2.cloned.1.call-update) | async-done | bytes 8388624 | tf_op jit(solution)/shard_map/all_gather | solution.py:34
  85.2 15.1 %fusion.2 = f32[2,1024,512]{1,2,0:T(8,128)} fusion(bf16[2,512,4096]{2,1,0:T(8,128)(2,1)} %all-gather.2.cloned.1.call-done, bf16[1024,4096]{1,0:T(8,128)(2,1)} %param.3), kind=kOutput, calls=%fused_computation.2 | convolution fusion | flops 8589934592 | bytes 20971520 | tf_op jit(solution)/shard_map/rf,kcf->krc/dot_general | solution.py:31
  100.2 0.0 reduce-scatter.3.cloned.1.call-update
  100.2 0.0 reduce-scatter.5.cloned.1.call-start
  100.3 50.8 %reduce-scatter.3.cloned.1.call-done = f32[2,128,512]{1,2,0:T(8,128)} async-done(((f32[2,1024,512]{1,2,0:T(8,128)}), f32[2,128,512]{1,2,0:T(8,128)}) %reduce-scatter.3.cloned.1.call-update) | async-done | bytes 524304 | tf_op jit(solution)/shard_map/reduce_scatter | solution.py:37
  151.1 1.1 fusion.10
  152.2 0.1 copy.4
  152.4 0.1 broadcast_in_dim.9
  152.5 18.3 %all_to_all.5 = bf16[8,128,512]{2,1,0:T(8,128)(2,1)S(1)} all-to-all(bf16[8,128,512]{2,1,0:T(8,128)(2,1)S(1)} %broadcast_in_dim.9), channel_id=1, replica_groups=mesh['img'=16,'feat'=8] {'feat'}, dimensions={0} | all-to-all | bytes 2097152 | tf_op jit(solution)/shard_map/all_to_all | solution.py:15
  170.8 10.1 %fusion.11 = f32[512,4096]{1,0:T(8,128)} fusion(bf16[1024,512]{1,0:T(8,128)(2,1)S(1)} %bitcast.15, bf16[1024,4096]{1,0:T(8,128)(2,1)} %param.3), kind=kOutput, calls=%fused_computation.13 | convolution fusion | flops 4294967296 | bytes 17825792 | tf_op jit(solution)/shard_map/dot_general | solution.py:40
  180.9 0.0 reduce-scatter.5.cloned.1.call-update
  181.0 101.6 %reduce-scatter.5.cloned.1.call-done = f32[32,4096]{1,0:T(8,128)} async-done(((f32[512,4096]{1,0:T(8,128)}), f32[32,4096]{1,0:T(8,128)}) %reduce-scatter.5.cloned.1.call-update) | async-done | bytes 524304 | tf_op jit(solution)/shard_map/reduce_scatter | solution.py:39
  282.6 1.9 broadcast_multiply_fusion
Async XLA Ops:
  6.5 78.6 %all-gather.2.cloned.1.call-start = ((), (), s32[]{:S(2)}) async-start(), calls=%async_computation.3 | async-start | bytes 8912896 | tf_op jit(solution)/shard_map/all_gather | solution.py:34
  8.4 142.7 %reduce-scatter.3.cloned.1.call-start = ((), (), s32[]{:S(2)}) async-start(), calls=%async_computation.4 | async-start | bytes 4718592 | tf_op jit(solution)/shard_map/reduce_scatter | solution.py:37
  100.2 182.4 %reduce-scatter.5.cloned.1.call-start = ((), (), s32[]{:S(2)}) async-start(), calls=%async_computation.5 | async-start | bytes 8912896 | tf_op jit(solution)/shard_map/reduce_scatter | solution.py:39
Sparse Core Ops, SparseCore 0:
  9.8 75.3 all-gather.1
  100.4 50.7 reduce-scatter.2
  181.1 101.4 reduce-scatter.4
where the time goes:
time: 291 us
  waiting for transfers between devices  229 us (79%)
  matrix products  25.2 us (9%)
  blocking collectives  18.3 us (6%)
  between operations  13.1 us (5%)
  other arithmetic  4.86 us (2%)
    reduce_scatter x1, waiting for transfers between devices, body(): lax.psum_scatter(lax.dot_general(curvature, features, (((0,), (0,)), ((),...  102 us
    all_gather x1, waiting for transfers between devices, body(): lax.all_gather(stacked, 'img', axis=1, tiled=True)  76.7 us
    reduce_scatter x1, waiting for transfers between devices, body(): lax.psum_scatter(partial_scores, 'feat', scatter_dimension=1, tiled=True)  50.8 us
    all_to_all x1, blocking collectives, from_everyone(): lax.all_to_all(jnp.broadcast_to(shard[None], (length, *shard.shape)), axi...  18.3 us
    dot_general x1, matrix products, body(): jnp.einsum('rf,kcf->krc', features, lax.all_gather(stacked, 'img', axis=1...  15.1 us
    dot_general x1, matrix products, body(): lax.dot_general(curvature, features, (((0,), (0,)), ((), ())), preferred_...  10.1 us
  transfers between devices with their start and end apart: 3, of which 3 were waited for; matrix products, arithmetic and copies ran while one was open for 0% of the time, Pallas kernels for 0%

commit v1 on v0

v1 whole, which is shorter than its diff:
```python
import jax
import jax.numpy as jnp
from jax import lax
from jax.experimental import pallas as pl
from jax.experimental.pallas import tpu as pltpu
from jax.sharding import PartitionSpec as P

ZS, YHS, CORES, YLS, XS = 4, 2, 2, 2, 4
CHUNKS = 4
COPIES = 31
PERIOD = 11.0
STAGES = (
    ("gather_start", 0.0),
    ("gather_second", 4.0),
    ("gather_forward", 8.0),
    ("gather_last", 12.0),
    ("scores", 14.0),
    ("scores_second", 20.0),
    ("scores_pair", 25.0),
    ("curvature", 28.0),
    ("curvature_second", 30.0),
    ("curvature_forward", 32.0),
    ("terms", 34.0),
    ("terms_first", 39.0),
    ("terms_second", 42.0),
    ("terms_pair", 45.0),
    ("terms_last", 48.0),
)


def order():
    events = []
    for place, (name, at) in enumerate(STAGES):
        for k in range(CHUNKS):
            lead = 0.0
            if place == 0:
                lead = -PERIOD + 3.0 if k else 0.0
            events.append((at + PERIOD * k + lead, place, k, name))
    return [(name, k) for _, _, k, name in sorted(events)]


def kernel(
    feat_hbm, w_hbm, d_hbm, out_ref,
    feat, w_ref, d_ref, gath, part, r1, r2, r3, curv, hess, r4,
    s5, r5, s6, r6, s7, r7,
    load, send, recv,
):
    f32, bf16 = jnp.float32, jnp.bfloat16
    img, col = lax.axis_index("img"), lax.axis_index("feat")
    core = lax.rem(img, CORES)
    yh = lax.rem(img // CORES, YHS)
    z = img // (CORES * YHS)
    x = lax.rem(col, XS)
    yl = col // XS
    z_up, z_down, z_far = lax.rem(z + 1, ZS), lax.rem(z + 3, ZS), lax.rem(z + 2, ZS)
    x_up, x_down, x_far = lax.rem(x + 1, XS), lax.rem(x + 3, XS), lax.rem(x + 2, XS)

    def at(z=z, yh=yh, core=core, yl=yl, x=x):
        return {"img": (z * YHS + yh) * CORES + core, "feat": yl * XS + x}

    to_z_up, to_z_down = at(z=z_up), at(z=z_down)
    to_x_up, to_x_down = at(x=x_up), at(x=x_down)
    to_yh, to_core, to_yl = at(yh=1 - yh), at(core=1 - core), at(yl=1 - yl)

    loads = [
        pltpu.make_async_copy(w_hbm, w_ref, load.at[0]),
        pltpu.make_async_copy(d_hbm, d_ref, load.at[1]),
        pltpu.make_async_copy(feat_hbm, feat, load.at[2]),
    ]
    for one in loads:
        one.start()
    barrier = pltpu.get_barrier_semaphore()
    partners = (to_z_up, to_z_down, to_x_up, to_x_down, to_yh, to_core, to_yl)
    for partner in partners:
        pl.semaphore_signal(
            barrier, inc=1, device_id=partner, device_id_type=pl.DeviceIdType.MESH
        )

    started = {}

    def push(k, number, src, dst, device):
        one = pltpu.make_async_remote_copy(
            src_ref=src,
            dst_ref=dst,
            send_sem=send.at[k, number],
            recv_sem=recv.at[k, number],
            device_id=device,
            device_id_type=pl.DeviceIdType.MESH,
        )
        one.start()
        started[k, number] = one

    def arrived(k, *numbers):
        for number in numbers:
            started[k, number].wait_recv()

    def same(k, number, ref, device):
        push(k, number, ref, ref, device)

    class Steps:
        def pack(k):
            rows = pl.ds(8 * k, 8)
            both = jnp.concatenate(
                (w_ref[...].astype(f32)[8 * k : 8 * k + 8], d_ref[...].astype(f32)[8 * k : 8 * k + 8]),
                axis=0,
            )
            gath[k, z, yh, core] = both.astype(bf16)

        def gather_start(k):
            mine = gath.at[k, z, yh, core]
            same(k, 0, mine, to_yh)
            same(k, 1, mine, to_z_up)
            same(k, 2, mine, to_z_down)
            same(k, 7, mine, to_core)

        def gather_second(k):
            arrived(k, 0)
            theirs = gath.at[k, z, 1 - yh, core]
            same(k, 3, theirs, to_z_up)
            same(k, 4, theirs, to_z_down)
            same(k, 8, theirs, to_core)

        def gather_forward(k):
            arrived(k, 1, 3)
            same(k, 5, gath.at[k, z_down, 0, core], to_z_up)
            arrived(k, 2, 4)
            same(k, 6, gath.at[k, z_up, 1, core], to_z_down)
            same(k, 9, gath.at[k, z_down, :, core], to_core)
            same(k, 10, gath.at[k, z_up, :, core], to_core)

        def gather_last(k):
            arrived(k, 5)
            same(k, 11, gath.at[k, z_far, 0, core], to_core)
            arrived(k, 6)
            same(k, 12, gath.at[k, z_far, 1, core], to_core)

        def scores(k):
            if k == 0:
                loads[2].wait()
            arrived(k, 7, 8, 9, 10, 11, 12)
            rows, depth = feat.shape
            tile = 256

            @pl.loop(0, rows // tile)
            def _(n):
                here = pl.ds(pl.multiple_of(n * tile, tile), tile)
                both = lax.dot_general(
                    gath[k].reshape(-1, depth),
                    feat[here, :],
                    (((1,), (1,)), ((), ())),
                    preferred_element_type=f32,
                )
                part[k, :, :, :, here] = both.reshape(YLS, XS, -1, tile)

            push(k, 13, part.at[k, 0, x_far], r1.at[k, 0], to_x_up)
            push(k, 14, part.at[k, 1, x_far], r1.at[k, 1], to_x_down)

        def scores_second(k):
            arrived(k, 13)
            part[k, 0, x_up] += r1[k, 0]
            push(k, 15, part.at[k, :, x_up], r2.at[k, 0], to_x_up)
            arrived(k, 14)
            part[k, 1, x_down] += r1[k, 1]
            push(k, 16, part.at[k, :, x_down], r2.at[k, 1], to_x_down)

        def scores_pair(k):
            arrived(k, 15, 16)
            part[k, 1 - yl, x] += r2[k, 0, 1 - yl] + r2[k, 1, 1 - yl]
            push(k, 17, part.at[k, 1 - yl, x], r3.at[k], to_yl)
            part[k, yl, x] += r2[k, 0, yl] + r2[k, 1, yl]

        def curvature(k):
            arrived(k, 17)
            total = part[k, yl, x] + r3[k]
            pair = total.reshape(2, 2, 8, total.shape[-1])
            prob = jax.nn.sigmoid(pair[:, 0])
            value = prob * (1.0 - prob) * pair[:, 1]
            curv[k, yl, x] = value.reshape(16, value.shape[-1]).astype(bf16)
            mine = curv.at[k, yl, x]
            same(k, 18, mine, to_yl)
            same(k, 19, mine, to_x_up)
            same(k, 20, mine, to_x_down)

        def curvature_second(k):
            arrived(k, 18)
            theirs = curv.at[k, 1 - yl, x]
            same(k, 21, theirs, to_x_up)
            same(k, 22, theirs, to_x_down)

        def curvature_forward(k):
            arrived(k, 19, 21)
            same(k, 23, curv.at[k, 0, x_down], to_x_up)
            arrived(k, 20, 22)
            same(k, 24, curv.at[k, 1, x_up], to_x_down)

        def terms(k):
            arrived(k, 23, 24)
            rows, depth = feat.shape
            tile = 512

            @pl.loop(0, depth // tile)
            def _(n):
                here = pl.ds(pl.multiple_of(n * tile, tile), tile)
                term = jnp.dot(
                    curv[k].reshape(-1, rows), feat[:, here], preferred_element_type=f32
                )
                hess[k, :, :, :, :, here] = term.reshape(ZS, YHS, CORES, 8, tile)

            push(k, 25, hess.at[k, :, :, 1 - core], r4.at[k], to_core)

        def chip(k, place):
            both = hess[k, place, :, core] + r4[k, place]
            return both.reshape(16, both.shape[-1])

        def terms_first(k):
            arrived(k, 25)
            s5[k] = Steps.chip(k, z_far).astype(bf16)
            half = s5.shape[-1] // 2
            push(k, 26, s5.at[k, :, pl.ds(0, half)], r5.at[k, 0], to_z_up)
            push(k, 27, s5.at[k, :, pl.ds(half, half)], r5.at[k, 1], to_z_down)

        def terms_second(k):
            half = s5.shape[-1] // 2
            arrived(k, 26)
            up = Steps.chip(k, z_up)
            s6[k, 0, :, :half] = (up[:, :half] + r5[k, 0].astype(f32)).astype(bf16)
            s6[k, 0, :, half:] = up[:, half:].astype(bf16)
            push(k, 28, s6.at[k, 0], r6.at[k, 0], to_z_up)
            arrived(k, 27)
            down = Steps.chip(k, z_down)
            s6[k, 1, :, :half] = down[:, :half].astype(bf16)
            s6[k, 1, :, half:] = (down[:, half:] + r5[k, 1].astype(f32)).astype(bf16)
            push(k, 29, s6.at[k, 1], r6.at[k, 1], to_z_down)

        def terms_pair(k):
            arrived(k, 28, 29)
            own = Steps.chip(k, z) + r6[k, 0].astype(f32) + r6[k, 1].astype(f32)
            half = own.shape[-1] // 2
            first = yh == 0
            mine = jnp.where(first, own[:8], own[8:])
            theirs = jnp.where(first, own[8:], own[:8])
            s7[k] = jnp.concatenate((theirs[:, :half], theirs[:, half:]), axis=0).astype(bf16)
            push(k, 30, s7.at[k], r7.at[k], to_yh)
            out_ref[8 * k : 8 * k + 8, :] = mine

        def terms_last(k):
            arrived(k, 30)
            other = r7[k].astype(f32)
            half = other.shape[-1]
            rows = slice(8 * k, 8 * k + 8)
            out_ref[rows, :half] = 4.0 * (out_ref[rows, :half] + other[:8])
            out_ref[rows, half:] = 4.0 * (out_ref[rows, half:] + other[8:])

    loads[0].wait()
    loads[1].wait()
    for k in range(CHUNKS):
        Steps.pack(k)
    pl.semaphore_wait(barrier, len(partners))
    for name, k in order():
        getattr(Steps, name)(k)
    for one in started.values():
        one.wait_send()


def body(features, weights, direction):
    rows, depth = features.shape
    mine = weights.shape[0]
    K = CHUNKS
    f32, bf16 = jnp.float32, jnp.bfloat16
    vmem = pltpu.VMEM
    return pl.pallas_call(
        kernel,
        out_shape=jax.ShapeDtypeStruct((mine, depth), f32),
        in_specs=[pl.BlockSpec(memory_space=pl.ANY)] * 3,
        out_specs=pl.BlockSpec(memory_space=vmem),
        scratch_shapes=[
            vmem((rows, depth), bf16),
            vmem((mine, depth), bf16),
            vmem((mine, depth), bf16),
            vmem((K, ZS, YHS, CORES, 16, depth), bf16),
            vmem((K, YLS, XS, 32, rows), f32),
            vmem((K, 2, 32, rows), f32),
            vmem((K, 2, YLS, 32, rows), f32),
            vmem((K, 32, rows), f32),
            vmem((K, YLS, XS, 16, rows), bf16),
            vmem((K, ZS, YHS, CORES, 8, depth), f32),
            vmem((K, ZS, YHS, 8, depth), f32),
            vmem((K, 16, depth), bf16),
            vmem((K, 2, 16, depth // 2), bf16),
            vmem((K, 2, 16, depth), bf16),
            vmem((K, 2, 16, depth), bf16),
            vmem((K, 16, depth // 2), bf16),
            vmem((K, 16, depth // 2), bf16),
            pltpu.SemaphoreType.DMA((3,)),
            pltpu.SemaphoreType.DMA((K, COPIES)),
            pltpu.SemaphoreType.DMA((K, COPIES)),
        ],
        compiler_params=pltpu.CompilerParams(
            collective_id=0, has_side_effects=True, vmem_limit_bytes=62 * 2**20
        ),
    )(features, weights, direction)


def solution(mesh):
    placed = (P("img", "feat"), P("img", "feat"), P("img", "feat"))
    return jax.shard_map(
        body, mesh=mesh, in_specs=placed, out_specs=P("img", "feat"), check_vma=False
    )
```

time: 291 us -> 138 us (0.47)
  waiting for transfers between devices: 229 us -> 0 us
  Pallas kernels: 0 us -> 135 us
  matrix products: 25.2 us -> 0 us
  blocking collectives: 18.3 us -> 0 us
  between operations: 13.1 us -> 0.01 us
  other arithmetic: 4.86 us -> 0 us
    reduce_scatter x2 -> x0, waiting for transfers between devices: 152 us -> none  [the longest x1 102 us: body(): lax.psum_scatter(lax.dot_general(curvature, features, (((0,), (0,)), ((),...]
    pallas_call x0 -> x1, Pallas kernels: none -> 135 us  [body(): pl.pallas_call(kernel, out_shape=jax.ShapeDtypeStruct((mine, depth), f32)...]
    all_gather x1 -> x0, waiting for transfers between devices: 76.7 us -> none  [body(): lax.all_gather(stacked, 'img', axis=1, tiled=True)]
    dot_general x2 -> x0, matrix products: 25.2 us -> none  [the longest x1 15.1 us: body(): jnp.einsum('rf,kcf->krc', features, lax.all_gather(stacked, 'img', axis=1...]
    all_to_all x1 -> x0, blocking collectives: 18.3 us -> none  [from_everyone(): lax.all_to_all(jnp.broadcast_to(shard[None], (length, *shard.shape)), axi...]
  transfers between devices with their start and end apart: 3 -> 0, of which waited for: 3 -> 0; matrix products, arithmetic and copies ran while one was open for 0% -> 0% of each run, Pallas kernels for 0% -> 0%
where the time goes in v1:
time: 138 us; the launch traced here: 137 us
  Pallas kernels  135 us (98%)
  local copies, waits for them, and re-layouts  1.87 us (1%)
    pallas_call x1, Pallas kernels, body(): pl.pallas_call(kernel, out_shape=jax.ShapeDtypeStruct((mine, depth), f32)...  135 us

profile of v1, /device:TPU:0, one launch (start us, length us, event | category | flops | bytes accessed | tf_op | source)
XLA Modules:
  0.0 137.0 jit_solution(17736294680135809389)
XLA Ops:
  0.0 135.1 %shard_map.37 = f32[32,4096]{1,0:T(8,128)} custom-call(bf16[1024,4096]{1,0:T(8,128)(2,1)} %feat_hbm.1, bf16[32,4096]{1,0:T(8,128)(2,1)} %w_hbm.1, bf16[32,4096]{1,0:T(8,128)(2,1)} %d_hbm.1), custom_call_target="tpu_custom_call" | custom-call | tf_op jit(solution)/shard_map/pallas_call | solution.py:271
  135.1 1.9 %copy.5 = f32[32,4096]{1,0:T(8,128)} copy(f32[32,4096]{1,0:T(8,128)} %shard_map.37) | data formatting | bytes 1048576

commit v2 on v0

v2 whole, which is shorter than its diff:
```python
import jax
import jax.numpy as jnp
from jax import lax
from jax.experimental import pallas as pl
from jax.experimental.pallas import tpu as pltpu
from jax.sharding import PartitionSpec as P

ZS, YHS, CORES, YLS, XS = 4, 2, 2, 2, 4
CHUNKS = 4
PIECES = 2
COPIES = 31
NAMES = (
    "gather_start", "gather_second", "gather_forward", "gather_last",
    "scores", "scores_second", "scores_pair", "curvature", "", "",
    "terms", "terms_first", "", "terms_pair", "terms_last",
)
ORDER = (
    (0, 0, 0), (0, 0, 1), (0, 1, 0), (1, 0, 0), (1, 0, 1), (0, 1, 1), (2, 0, 0),
    (2, 0, 1), (3, 0, 0), (1, 1, 1), (0, 2, 0), (1, 1, 0), (0, 2, 1), (3, 0, 1),
    (4, 0, 0), (2, 1, 1), (5, 0, 0), (2, 1, 0), (1, 2, 1), (0, 3, 0), (3, 1, 1),
    (0, 3, 1), (1, 2, 0), (3, 1, 0), (5, 0, 1), (6, 0, 0), (4, 1, 0), (1, 3, 1),
    (6, 0, 1), (2, 2, 1), (7, 0, 0), (5, 1, 0), (2, 2, 0), (3, 2, 1), (5, 1, 1),
    (1, 3, 0), (7, 0, 1), (3, 2, 0), (6, 1, 0), (2, 3, 0), (2, 3, 1), (4, 2, 0),
    (7, 1, 0), (3, 3, 1), (6, 1, 1), (5, 2, 0), (3, 3, 0), (10, 0, 0), (7, 1, 1),
    (4, 3, 0), (6, 2, 0), (5, 2, 1), (11, 0, 1), (11, 0, 0), (5, 3, 0), (10, 1, 0),
    (11, 1, 0), (5, 3, 1), (7, 2, 0), (6, 2, 1), (6, 3, 0), (7, 2, 1), (6, 3, 1),
    (13, 0, 0), (7, 3, 0), (7, 3, 1), (11, 1, 1), (10, 2, 0), (11, 2, 0), (13, 0, 1),
    (13, 1, 1), (11, 2, 1), (10, 3, 0), (11, 3, 0), (14, 0, 1), (13, 2, 0), (13, 1, 0),
    (14, 1, 1), (11, 3, 1), (13, 3, 0), (13, 2, 1), (13, 3, 1), (14, 3, 0), (14, 2, 0),
    (14, 1, 0), (14, 2, 1), (14, 0, 0), (14, 3, 1),
)


def kernel(
    feat_hbm, w_hbm, d_hbm, out_hbm,
    feat, w_ref, d_ref, gath, part, r1, r2, r3, curv, hess, r4,
    zs, zr, ys, yr, out,
    load, store, send, recv,
):
    f32, bf16 = jnp.float32, jnp.bfloat16
    mesh_ids = pl.DeviceIdType.MESH
    img, col = lax.axis_index("img"), lax.axis_index("feat")
    core = lax.rem(img, CORES)
    yh = lax.rem(img // CORES, YHS)
    z = img // (CORES * YHS)
    x = lax.rem(col, XS)
    yl = col // XS
    z_up, z_down, z_far = lax.rem(z + 1, ZS), lax.rem(z + 3, ZS), lax.rem(z + 2, ZS)
    x_up, x_down, x_far = lax.rem(x + 1, XS), lax.rem(x + 3, XS), lax.rem(x + 2, XS)

    def at(z=z, yh=yh, core=core, yl=yl, x=x):
        return {"img": (z * YHS + yh) * CORES + core, "feat": yl * XS + x}

    to_z_up, to_z_down, to_z_far = at(z=z_up), at(z=z_down), at(z=z_far)
    to_x_up, to_x_down, to_x_far = at(x=x_up), at(x=x_down), at(x=x_far)
    to_yh, to_core, to_yl = at(yh=1 - yh), at(core=1 - core), at(yl=1 - yl)
    across = [at(yl=1 - yl, x=one) for one in (x_up, x_down, x_far)]

    loads = [
        pltpu.make_async_copy(w_hbm, w_ref, load.at[0]),
        pltpu.make_async_copy(d_hbm, d_ref, load.at[1]),
        pltpu.make_async_copy(feat_hbm, feat, load.at[2]),
    ]
    for one in loads:
        one.start()
    barrier = pltpu.get_barrier_semaphore()
    partners = [
        to_core, to_yl, to_z_up, to_z_down, to_x_up, to_x_down,
        to_yh, to_z_far, to_x_far, *across,
    ]
    for partner in partners:
        pl.semaphore_signal(barrier, inc=1, device_id=partner, device_id_type=mesh_ids)

    rows, depth = feat.shape
    wide, long = depth // PIECES, rows // PIECES
    started, stores = {}, []

    def lanes(p):
        return pl.ds(p * wide, wide)

    def images(p):
        return pl.ds(p * long, long)

    def push(k, p, number, src, dst, device):
        one = pltpu.make_async_remote_copy(
            src_ref=src,
            dst_ref=dst,
            send_sem=send.at[k, p, number],
            recv_sem=recv.at[k, p, number],
            device_id=device,
            device_id_type=mesh_ids,
        )
        one.start()
        started[k, p, number] = one

    def arrived(k, p, *numbers):
        for number in numbers:
            started[k, p, number].wait_recv()

    def same(k, p, number, ref, device):
        push(k, p, number, ref, ref, device)

    def pack(k):
        both = jnp.concatenate(
            (
                w_ref[...].astype(f32)[8 * k : 8 * k + 8],
                d_ref[...].astype(f32)[8 * k : 8 * k + 8],
            ),
            axis=0,
        )
        gath[k, z, yh, core] = both.astype(bf16)

    def gather_start(k, p):
        if p == 0 and k > 0:
            pack(k)
        mine = gath.at[k, z, yh, core, :, lanes(p)]
        same(k, p, 0, mine, to_yh)
        same(k, p, 1, mine, to_z_up)
        same(k, p, 2, mine, to_z_down)
        same(k, p, 7, mine, to_core)

    def gather_second(k, p):
        arrived(k, p, 0)
        theirs = gath.at[k, z, 1 - yh, core, :, lanes(p)]
        same(k, p, 3, theirs, to_z_up)
        same(k, p, 4, theirs, to_z_down)
        same(k, p, 8, theirs, to_core)

    def gather_forward(k, p):
        arrived(k, p, 1, 3)
        same(k, p, 5, gath.at[k, z_down, 0, core, :, lanes(p)], to_z_up)
        arrived(k, p, 2, 4)
        same(k, p, 6, gath.at[k, z_up, 1, core, :, lanes(p)], to_z_down)
        same(k, p, 9, gath.at[k, z_down, :, core, :, lanes(p)], to_core)
        same(k, p, 10, gath.at[k, z_up, :, core, :, lanes(p)], to_core)

    def gather_last(k, p):
        arrived(k, p, 5)
        same(k, p, 11, gath.at[k, z_far, 0, core, :, lanes(p)], to_core)
        arrived(k, p, 6)
        same(k, p, 12, gath.at[k, z_far, 1, core, :, lanes(p)], to_core)

    def scores(k, _):
        if started.pop("features", None):
            loads[2].wait()
        for p in range(PIECES):
            arrived(k, p, 7, 8, 9, 10, 11, 12)
        for p in range(PIECES):
            both = lax.dot_general(
                gath[k].reshape(-1, depth),
                feat[images(p), :],
                (((1,), (1,)), ((), ())),
                preferred_element_type=f32,
            )
            part[k, :, :, :, images(p)] = both.reshape(YLS, XS, -1, long)
            push(k, p, 13, part.at[k, 0, x_far, :, images(p)], r1.at[k, p, 0], to_x_up)
            push(k, p, 14, part.at[k, 1, x_far, :, images(p)], r1.at[k, p, 1], to_x_down)

    def scores_second(k, p):
        here = images(p)
        arrived(k, p, 13)
        part[k, 0, x_up, :, here] += r1[k, p, 0]
        push(k, p, 15, part.at[k, :, x_up, :, here], r2.at[k, p, 0], to_x_up)
        arrived(k, p, 14)
        part[k, 1, x_down, :, here] += r1[k, p, 1]
        push(k, p, 16, part.at[k, :, x_down, :, here], r2.at[k, p, 1], to_x_down)

    def scores_pair(k, p):
        here = images(p)
        arrived(k, p, 15, 16)
        part[k, 1 - yl, x, :, here] += r2[k, p, 0, 1 - yl] + r2[k, p, 1, 1 - yl]
        push(k, p, 17, part.at[k, 1 - yl, x, :, here], r3.at[k, p], to_yl)
        part[k, yl, x, :, here] += r2[k, p, 0, yl] + r2[k, p, 1, yl]

    def curvature(k, p):
        here = images(p)
        arrived(k, p, 17)
        total = part[k, yl, x, :, here] + r3[k, p]
        pair = total.reshape(2, 2, 8, long)
        prob = jax.nn.sigmoid(pair[:, 0])
        value = prob * (1.0 - prob) * pair[:, 1]
        curv[k, yl, x, :, here] = value.reshape(16, long).astype(bf16)
        mine = curv.at[k, yl, x, :, here]
        for number, device in enumerate((to_yl, to_x_up, to_x_down, *across, to_x_far), 18):
            same(k, p, number, mine, device)

    def terms(k, _):
        for p in range(PIECES):
            arrived(k, p, *range(18, 25))
        tile = 1024
        for p in range(PIECES):

            @pl.loop(0, wide // tile)
            def _(n):
                here = pl.ds(pl.multiple_of(p * wide + n * tile, tile), tile)
                term = jnp.dot(
                    curv[k].reshape(-1, rows), feat[:, here], preferred_element_type=f32
                )
                hess[k, :, :, :, :, here] = term.reshape(ZS, YHS, CORES, 8, tile)

            push(
                k, p, 25, hess.at[k, :, :, 1 - core, :, lanes(p)], r4.at[k, :, :, :, lanes(p)], to_core
            )

    def chip(k, p, place):
        here = lanes(p)
        both = hess[k, place, :, core, :, here] + r4[k, place, :, :, here]
        return both.reshape(16, wide)

    def terms_first(k, p):
        arrived(k, p, 25)
        there = ((26, z_far, to_z_far), (28, z_up, to_z_up), (29, z_down, to_z_down))
        for slot, (number, place, device) in enumerate(there):
            zs[k, p, slot] = chip(k, p, place).astype(bf16)
            push(k, p, number, zs.at[k, p, slot], zr.at[k, p, slot], device)

    def terms_pair(k, p):
        arrived(k, p, 26, 28, 29)
        own = chip(k, p, z)
        for slot in range(3):
            own = own + zr[k, p, slot].astype(f32)
        half = wide // 2
        first = yh == 0
        mine = jnp.where(first, own[:8], own[8:])
        theirs = jnp.where(first, own[8:], own[:8])
        ys[k, p] = jnp.concatenate((theirs[:, :half], theirs[:, half:]), axis=0).astype(bf16)
        push(k, p, 30, ys.at[k, p], yr.at[k, p], to_yh)
        out[k, :, lanes(p)] = mine

    def terms_last(k, p):
        arrived(k, p, 30)
        other = yr[k, p].astype(f32)
        both = jnp.concatenate((other[:8], other[8:]), axis=1)
        out[k, :, lanes(p)] = 4.0 * (out[k, :, lanes(p)] + both)
        there = out_hbm.at[pl.ds(8 * k, 8), lanes(p)]
        one = pltpu.make_async_copy(out.at[k, :, lanes(p)], there, store.at[k, p])
        one.start()
        stores.append(one)

    steps = {one.__name__: one for one in (
        gather_start, gather_second, gather_forward, gather_last, scores, scores_second,
        scores_pair, curvature, terms, terms_first, terms_pair, terms_last,
    )}
    started["features"] = True
    loads[0].wait()
    loads[1].wait()
    pack(0)
    pl.semaphore_wait(barrier, len(partners))
    for place, k, p in ORDER:
        steps[NAMES[place]](k, p)
    for one in started.values():
        one.wait_send()
    for one in stores:
        one.wait()


def body(features, weights, direction):
    rows, depth = features.shape
    mine = weights.shape[0]
    K, Q = CHUNKS, PIECES
    wide, long = depth // Q, rows // Q
    f32, bf16 = jnp.float32, jnp.bfloat16
    vmem = pltpu.VMEM
    return pl.pallas_call(
        kernel,
        out_shape=jax.ShapeDtypeStruct((mine, depth), f32),
        in_specs=[pl.BlockSpec(memory_space=pl.ANY)] * 3,
        out_specs=pl.BlockSpec(memory_space=pl.ANY),
        scratch_shapes=[
            vmem((rows, depth), bf16),
            vmem((mine, depth), bf16),
            vmem((mine, depth), bf16),
            vmem((K, ZS, YHS, CORES, 16, depth), bf16),
            vmem((K, YLS, XS, 32, rows), f32),
            vmem((K, Q, 2, 32, long), f32),
            vmem((K, Q, 2, YLS, 32, long), f32),
            vmem((K, Q, 32, long), f32),
            vmem((K, YLS, XS, 16, rows), bf16),
            vmem((K, ZS, YHS, CORES, 8, depth), f32),
            vmem((K, ZS, YHS, 8, depth), f32),
            vmem((K, Q, 3, 16, wide), bf16),
            vmem((K, Q, 3, 16, wide), bf16),
            vmem((K, Q, 16, wide // 2), bf16),
            vmem((K, Q, 16, wide // 2), bf16),
            vmem((K, 8, depth), f32),
            pltpu.SemaphoreType.DMA((3,)),
            pltpu.SemaphoreType.DMA((K, Q)),
            pltpu.SemaphoreType.DMA((K, Q, COPIES)),
            pltpu.SemaphoreType.DMA((K, Q, COPIES)),
        ],
        compiler_params=pltpu.CompilerParams(
            collective_id=0, has_side_effects=True, vmem_limit_bytes=62 * 2**20
        ),
    )(features, weights, direction)


def solution(mesh):
    placed = (P("img", "feat"), P("img", "feat"), P("img", "feat"))
    return jax.shard_map(
        body, mesh=mesh, in_specs=placed, out_specs=P("img", "feat"), check_vma=False
    )
```

time: 291 us -> 101 us (0.35)
  waiting for transfers between devices: 229 us -> 0 us
  Pallas kernels: 0 us -> 99.2 us
  matrix products: 25.2 us -> 0 us
  blocking collectives: 18.3 us -> 0 us
  between operations: 13.1 us -> 0.01 us
  other arithmetic: 4.86 us -> 0 us
    reduce_scatter x2 -> x0, waiting for transfers between devices: 152 us -> none  [the longest x1 102 us: body(): lax.psum_scatter(lax.dot_general(curvature, features, (((0,), (0,)), ((),...]
    pallas_call x0 -> x1, Pallas kernels: none -> 99.2 us  [body(): pl.pallas_call(kernel, out_shape=jax.ShapeDtypeStruct((mine, depth), f32)...]
    all_gather x1 -> x0, waiting for transfers between devices: 76.7 us -> none  [body(): lax.all_gather(stacked, 'img', axis=1, tiled=True)]
    dot_general x2 -> x0, matrix products: 25.2 us -> none  [the longest x1 15.1 us: body(): jnp.einsum('rf,kcf->krc', features, lax.all_gather(stacked, 'img', axis=1...]
    all_to_all x1 -> x0, blocking collectives: 18.3 us -> none  [from_everyone(): lax.all_to_all(jnp.broadcast_to(shard[None], (length, *shard.shape)), axi...]
  transfers between devices with their start and end apart: 3 -> 0, of which waited for: 3 -> 0; matrix products, arithmetic and copies ran while one was open for 0% -> 0% of each run, Pallas kernels for 0% -> 0%
where the time goes in v2:
time: 101 us
  Pallas kernels  99.2 us (98%)
  local copies, waits for them, and re-layouts  1.87 us (2%)
    pallas_call x1, Pallas kernels, body(): pl.pallas_call(kernel, out_shape=jax.ShapeDtypeStruct((mine, depth), f32)...  99.2 us

profile of v2, /device:TPU:0, one launch (start us, length us, event | category | flops | bytes accessed | tf_op | source)
XLA Modules:
  0.0 101.0 jit_solution(9429381722299585368)
XLA Ops:
  0.0 99.2 %shard_map.37 = f32[32,4096]{1,0:T(8,128)} custom-call(bf16[1024,4096]{1,0:T(8,128)(2,1)} %feat_hbm.1, bf16[32,4096]{1,0:T(8,128)(2,1)} %w_hbm.1, bf16[32,4096]{1,0:T(8,128)(2,1)} %d_hbm.1), custom_call_target="tpu_custom_call" | custom-call | tf_op jit(solution)/shard_map/pallas_call | solution.py:264
  99.2 1.9 %copy.5 = f32[32,4096]{1,0:T(8,128)} copy(f32[32,4096]{1,0:T(8,128)} %shard_map.37) | data formatting | bytes 1048576

commit v3 on v2

v3 whole, which is shorter than its diff:
```python
import jax
import jax.numpy as jnp
from jax import lax
from jax.experimental import pallas as pl
from jax.experimental.pallas import tpu as pltpu
from jax.sharding import PartitionSpec as P

ZS, YHS, CORES, YLS, XS = 4, 2, 2, 2, 4
CHUNKS = 4
PIECES = 2
BY_PIECE = {0: 0, 1: 1, 3: 1, 2: 2, 4: 2, 5: 3, 6: 4, 13: 5, 14: 6, 15: 7, 16: 7, 17: 8}
BY_PIECE |= {25: 9, 26: 10, 28: 10, 29: 10, 31: 11}
BY_CHUNK = {7: 0, 8: 0, 9: 0, 10: 0, 11: 0, 12: 0, 18: 1, 21: 1, 22: 1, 23: 1, 19: 2, 20: 3, 24: 4}
SENDS = 64
PAIRED = (2, 3)
NAMES = (
    "gather_start", "gather_second", "gather_forward", "gather_last",
    "scores", "scores_far", "scores_second", "scores_pair", "curvature", "", "",
    "terms", "terms_first", "", "terms_pair",
)
ORDER = (
    (0, 0, 0, 0), (0, 0, 1, 0), (0, 1, 0, 0), (1, 0, 0, 0), (1, 0, 1, 0), (1, 1, 0, 4),
    (2, 0, 0, 4), (2, 0, 1, 4), (0, 1, 1, 0), (2, 1, 0, 3), (3, 0, 0, 3), (1, 1, 1, 3),
    (0, 2, 0, 0), (3, 0, 1, 3), (4, 0, 0, 1), (4, 0, 1, 0), (2, 1, 1, 8), (3, 1, 0, 0),
    (0, 2, 1, 0), (6, 0, 0, 6), (1, 2, 0, 0), (6, 0, 1, 4), (3, 1, 1, 1), (1, 2, 1, 6),
    (4, 1, 0, 0), (2, 2, 0, 3), (7, 0, 0, 0), (4, 1, 1, 0), (2, 2, 1, 0), (0, 3, 0, 0),
    (0, 3, 1, 0), (8, 0, 0, 14), (7, 0, 1, 0), (3, 2, 0, 0), (6, 1, 0, 0), (3, 2, 1, 5),
    (1, 3, 0, 2), (4, 2, 0, 5), (1, 3, 1, 0), (6, 1, 1, 0), (4, 2, 1, 0), (2, 3, 0, 7),
    (5, 2, 0, 16), (8, 0, 1, 0), (2, 3, 1, 0), (5, 2, 1, 3), (3, 3, 0, 6), (7, 1, 1, 5),
    (6, 2, 0, 0), (7, 1, 0, 0), (3, 3, 1, 0), (4, 3, 0, 7), (6, 2, 1, 0), (8, 1, 0, 13),
    (4, 3, 1, 0), (5, 3, 0, 5), (7, 2, 0, 0), (8, 1, 1, 0), (11, 0, 0, 0), (11, 0, 1, 0),
    (5, 3, 1, 6), (6, 3, 0, 3), (12, 0, 0, 0), (7, 2, 1, 0), (6, 3, 1, 5), (8, 2, 0, 0),
    (11, 1, 0, 9), (8, 2, 1, 0), (11, 1, 1, 0), (12, 0, 1, 0), (12, 1, 0, 7), (7, 3, 0, 0),
    (7, 3, 1, 6), (12, 1, 1, 0), (8, 3, 1, 0), (11, 2, 0, 6), (8, 3, 0, 0), (11, 2, 1, 0),
    (14, 1, 0, 0), (14, 0, 0, 0), (14, 0, 1, 0), (12, 2, 0, 17), (12, 2, 1, 3), (11, 3, 0, 1),
    (14, 1, 1, 0), (12, 3, 0, 19), (11, 3, 1, 0), (12, 3, 1, 5), (14, 2, 1, 0), (14, 2, 0, 0),
    (14, 3, 0, 5), (14, 3, 1, 1),
)


def kernel(
    feat_hbm, w_hbm, d_hbm, mine_hbm, theirs_hbm,
    feat, w_ref, d_ref, gath, part, rf, r1, r2, r3, curv, hess, r4,
    zs, zr, ys, out,
    load, store, send, by_piece, by_chunk, last,
):
    f32, bf16 = jnp.float32, jnp.bfloat16
    mesh_ids = pl.DeviceIdType.MESH
    img, col = lax.axis_index("img"), lax.axis_index("feat")
    core = lax.rem(img, CORES)
    yh = lax.rem(img // CORES, YHS)
    z = img // (CORES * YHS)
    x = lax.rem(col, XS)
    yl = col // XS
    z_up, z_down, z_far = lax.rem(z + 1, ZS), lax.rem(z + 3, ZS), lax.rem(z + 2, ZS)
    x_up, x_down, x_far = lax.rem(x + 1, XS), lax.rem(x + 3, XS), lax.rem(x + 2, XS)

    def at(z=z, yh=yh, core=core, yl=yl, x=x):
        return {"img": (z * YHS + yh) * CORES + core, "feat": yl * XS + x}

    to_z_up, to_z_down, to_z_far = at(z=z_up), at(z=z_down), at(z=z_far)
    to_x_up, to_x_down, to_x_far = at(x=x_up), at(x=x_down), at(x=x_far)
    to_yh, to_core, to_yl = at(yh=1 - yh), at(core=1 - core), at(yl=1 - yl)
    across = [at(yl=1 - yl, x=one) for one in (x_up, x_down, x_far)]

    loads = [
        pltpu.make_async_copy(w_hbm, w_ref, load.at[0]),
        pltpu.make_async_copy(d_hbm, d_ref, load.at[1]),
        pltpu.make_async_copy(feat_hbm, feat, load.at[2]),
    ]
    for one in loads:
        one.start()
    barrier = pltpu.get_barrier_semaphore()
    partners = [
        to_core, to_yl, to_z_up, to_z_down, to_x_up, to_x_down,
        to_yh, to_z_far, to_x_far, *across,
    ]
    for partner in partners:
        pl.semaphore_signal(barrier, inc=1, device_id=partner, device_id_type=mesh_ids)

    rows, depth = feat.shape
    wide, long = depth // PIECES, rows // PIECES
    slots, flying, waiting = list(range(SENDS)), [], [loads[2]]

    def lanes(p):
        return pl.ds(p * wide, wide)

    def images(p):
        return pl.ds(p * long, long)

    def receive(k, p, number):
        if number in BY_PIECE:
            return by_piece.at[k, p, BY_PIECE[number]]
        return by_chunk.at[k, BY_CHUNK[number]] if number in BY_CHUNK else last.at[0]

    def retire():
        slot, one = flying.pop(0)
        one.wait_send()
        slots.append(slot)

    def push(k, p, number, src, dst, device):
        if not slots:
            retire()
        slot = slots.pop(0)
        one = pltpu.make_async_remote_copy(
            src_ref=src,
            dst_ref=dst,
            send_sem=send.at[slot],
            recv_sem=receive(k, p, number),
            device_id=device,
            device_id_type=mesh_ids,
        )
        one.start()
        flying.append((slot, one))

    def arrived(k, p, number, ref):
        pltpu.make_async_remote_copy(
            src_ref=ref,
            dst_ref=ref,
            send_sem=send.at[0],
            recv_sem=receive(k, p, number),
            device_id=to_core,
            device_id_type=mesh_ids,
        ).wait_recv()

    def same(k, p, number, ref, device):
        push(k, p, number, ref, ref, device)

    def pack(k):
        both = jnp.concatenate(
            (
                w_ref[...].astype(f32)[8 * k : 8 * k + 8],
                d_ref[...].astype(f32)[8 * k : 8 * k + 8],
            ),
            axis=0,
        )
        gath[k, z, yh, core] = both.astype(bf16)

    def gather_start(k, p):
        if p == 0 and k > 0:
            pack(k)
        mine = gath.at[k, z, yh, core, :, lanes(p)]
        same(k, p, 0, mine, to_yh)
        same(k, p, 1, mine, to_z_up)
        same(k, p, 2, mine, to_z_down)
        same(k, p, 7, mine, to_core)

    def gather_second(k, p):
        theirs = gath.at[k, z, 1 - yh, core, :, lanes(p)]
        arrived(k, p, 0, theirs)
        same(k, p, 3, theirs, to_z_up)
        same(k, p, 4, theirs, to_z_down)
        same(k, p, 8, theirs, to_core)

    def gather_forward(k, p):
        arrived(k, p, 1, gath.at[k, z_down, :, core, :, lanes(p)])
        same(k, p, 5, gath.at[k, z_down, 0, core, :, lanes(p)], to_z_up)
        arrived(k, p, 2, gath.at[k, z_up, :, core, :, lanes(p)])
        same(k, p, 6, gath.at[k, z_up, 1, core, :, lanes(p)], to_z_down)
        same(k, p, 9, gath.at[k, z_down, :, core, :, lanes(p)], to_core)
        same(k, p, 10, gath.at[k, z_up, :, core, :, lanes(p)], to_core)

    def gather_last(k, p):
        arrived(k, p, 5, gath.at[k, z_far, 0, core, :, lanes(p)])
        same(k, p, 11, gath.at[k, z_far, 0, core, :, lanes(p)], to_core)
        arrived(k, p, 6, gath.at[k, z_far, 1, core, :, lanes(p)])
        same(k, p, 12, gath.at[k, z_far, 1, core, :, lanes(p)], to_core)

    def scores(k, p):
        here = images(p)
        if waiting:
            waiting.pop().wait()
        if p == 0:
            arrived(k, p, 7, gath.at[k, :, :, 1 - core])
        both = lax.dot_general(
            gath[k].reshape(-1, depth),
            feat[here, :],
            (((1,), (1,)), ((), ())),
            preferred_element_type=f32,
        )
        part[k, :, :, :, here] = both.reshape(YLS, XS, -1, long)
        if k in PAIRED:
            push(k, p, 31, part.at[k, 1 - yl, x_far, :, here], rf.at[k, p], to_yl)
        else:
            push(k, p, 13, part.at[k, 0, x_far, :, here], r1.at[k, p, 0], to_x_up)
            push(k, p, 14, part.at[k, 1, x_far, :, here], r1.at[k, p, 1], to_x_down)

    def halves(p):
        half = long // 2
        return pl.ds(p * long, half), pl.ds(p * long + half, half), pl.ds(0, half)

    def scores_far(k, p):
        first, second, slot = halves(p)
        arrived(k, p, 31, rf.at[k, p])
        part[k, yl, x_far, :, images(p)] += rf[k, p]
        push(k, p, 13, part.at[k, yl, x_far, :, first], r1.at[k, p, 0, :, slot], to_x_up)
        push(k, p, 14, part.at[k, yl, x_far, :, second], r1.at[k, p, 1, :, slot], to_x_down)

    def scores_second(k, p):
        here = images(p)
        first, second, slot = halves(p)
        up = r1.at[k, p, 0, :, slot] if k in PAIRED else r1.at[k, p, 0]
        down = r1.at[k, p, 1, :, slot] if k in PAIRED else r1.at[k, p, 1]
        arrived(k, p, 13, up)
        if k in PAIRED:
            part[k, yl, x_up, :, first] += r1[k, p, 0, :, slot]
        else:
            part[k, 0, x_up, :, here] += r1[k, p, 0]
        push(k, p, 15, part.at[k, :, x_up, :, here], r2.at[k, p, 0], to_x_up)
        arrived(k, p, 14, down)
        if k in PAIRED:
            part[k, yl, x_down, :, second] += r1[k, p, 1, :, slot]
        else:
            part[k, 1, x_down, :, here] += r1[k, p, 1]
        push(k, p, 16, part.at[k, :, x_down, :, here], r2.at[k, p, 1], to_x_down)

    def scores_pair(k, p):
        here = images(p)
        arrived(k, p, 15, r2.at[k, p])
        part[k, 1 - yl, x, :, here] += r2[k, p, 0, 1 - yl] + r2[k, p, 1, 1 - yl]
        push(k, p, 17, part.at[k, 1 - yl, x, :, here], r3.at[k, p], to_yl)
        part[k, yl, x, :, here] += r2[k, p, 0, yl] + r2[k, p, 1, yl]

    def curvature(k, p):
        here = images(p)
        arrived(k, p, 17, r3.at[k, p])
        total = part[k, yl, x, :, here] + r3[k, p]
        pair = total.reshape(2, 2, 8, long)
        prob = jax.nn.sigmoid(pair[:, 0])
        value = prob * (1.0 - prob) * pair[:, 1]
        curv[k, yl, x, :, here] = value.reshape(16, long).astype(bf16)
        mine = curv.at[k, yl, x, :, here]
        for number, device in enumerate((to_yl, to_x_up, to_x_down, *across, to_x_far), 18):
            same(k, p, number, mine, device)

    def terms(k, p):
        if p == 0:
            arrived(k, p, 18, curv.at[k, 1 - yl])
            for number, place in ((19, x_down), (20, x_up), (24, x_far)):
                arrived(k, p, number, curv.at[k, yl, place])
        tile = 1024

        @pl.loop(0, wide // tile)
        def _(n):
            here = pl.ds(pl.multiple_of(p * wide + n * tile, tile), tile)
            term = jnp.dot(
                curv[k].reshape(-1, rows), feat[:, here], preferred_element_type=f32
            )
            hess[k, :, :, :, :, here] = term.reshape(ZS, YHS, CORES, 8, tile)

        there = lanes(p)
        push(k, p, 25, hess.at[k, :, :, 1 - core, :, there], r4.at[k, :, :, :, there], to_core)

    def chip(k, p, place):
        here = lanes(p)
        both = hess[k, place, :, core, :, here] + r4[k, place, :, :, here]
        return both.reshape(16, wide)

    def terms_first(k, p):
        arrived(k, p, 25, r4.at[k, :, :, :, lanes(p)])
        there = ((26, z_far, to_z_far), (28, z_up, to_z_up), (29, z_down, to_z_down))
        for slot, (number, place, device) in enumerate(there):
            zs[k, p, slot] = chip(k, p, place).astype(bf16)
            push(k, p, number, zs.at[k, p, slot], zr.at[k, p, slot], device)

    def terms_pair(k, p):
        arrived(k, p, 26, zr.at[k, p])
        own = chip(k, p, z)
        for slot in range(3):
            own = own + zr[k, p, slot].astype(f32)
        first = yh == 0
        ys[k, p] = jnp.where(first, own[8:], own[:8]).astype(bf16)
        push(k, p, 30, ys.at[k, p], theirs_hbm.at[k, :, lanes(p)], to_yh)
        out[k, p] = jnp.where(first, own[:8], own[8:])
        pltpu.make_async_copy(out.at[k, p], mine_hbm.at[k, :, lanes(p)], store.at[0]).start()

    steps = {one.__name__: one for one in (
        gather_start, gather_second, gather_forward, gather_last, scores, scores_far,
        scores_second, scores_pair, curvature, terms, terms_first, terms_pair,
    )}
    loads[0].wait()
    loads[1].wait()
    pack(0)
    pl.semaphore_wait(barrier, len(partners))
    for place, k, p, enough in ORDER:
        for _ in range(min(enough, len(flying))):
            retire()
        steps[NAMES[place]](k, p)
    arrived(0, 0, 30, theirs_hbm)
    pltpu.make_async_copy(mine_hbm, mine_hbm, store.at[0]).wait()
    while flying:
        retire()


def body(features, weights, direction):
    rows, depth = features.shape
    mine = weights.shape[0]
    K, Q = CHUNKS, PIECES
    wide, long = depth // Q, rows // Q
    f32, bf16 = jnp.float32, jnp.bfloat16
    vmem = pltpu.VMEM
    own, other = pl.pallas_call(
        kernel,
        out_shape=(
            jax.ShapeDtypeStruct((K, mine // K, depth), f32),
            jax.ShapeDtypeStruct((K, mine // K, depth), bf16),
        ),
        in_specs=[pl.BlockSpec(memory_space=pl.ANY)] * 3,
        out_specs=[pl.BlockSpec(memory_space=pl.ANY)] * 2,
        scratch_shapes=[
            vmem((rows, depth), bf16),
            vmem((mine, depth), bf16),
            vmem((mine, depth), bf16),
            vmem((K, ZS, YHS, CORES, 16, depth), bf16),
            vmem((K, YLS, XS, 32, rows), f32),
            vmem((K, Q, 32, long), f32),
            vmem((K, Q, 2, 32, long), f32),
            vmem((K, Q, 2, YLS, 32, long), f32),
            vmem((K, Q, 32, long), f32),
            vmem((K, YLS, XS, 16, rows), bf16),
            vmem((K, ZS, YHS, CORES, 8, depth), f32),
            vmem((K, ZS, YHS, 8, depth), f32),
            vmem((K, Q, 3, 16, wide), bf16),
            vmem((K, Q, 3, 16, wide), bf16),
            vmem((K, Q, 8, wide), bf16),
            vmem((K, Q, 8, wide), f32),
            pltpu.SemaphoreType.DMA((3,)),
            pltpu.SemaphoreType.DMA((1,)),
            pltpu.SemaphoreType.DMA((SENDS,)),
            pltpu.SemaphoreType.DMA((K, Q, 12)),
            pltpu.SemaphoreType.DMA((K, 5)),
            pltpu.SemaphoreType.DMA((1,)),
        ],
        compiler_params=pltpu.CompilerParams(
            collective_id=0, has_side_effects=True, vmem_limit_bytes=62 * 2**20
        ),
    )(features, weights, direction)
    return (4.0 * (own + other.astype(f32))).reshape(mine, depth)


def solution(mesh):
    placed = (P("img", "feat"), P("img", "feat"), P("img", "feat"))
    return jax.shard_map(
        body, mesh=mesh, in_specs=placed, out_specs=P("img", "feat"), check_vma=False
    )
```

time: 101 us -> 95.3 us (0.944)
  Pallas kernels: 99.2 us -> 93.3 us
  other arithmetic: 0 us -> 1.96 us
  local copies, waits for them, and re-layouts: 1.87 us -> 0 us
    pallas_call x1, Pallas kernels: 99.2 us -> 93.3 us  [body(): pl.pallas_call(kernel, out_shape=(jax.ShapeDtypeStruct((K, mine // K, dep...]
    reshape x0 -> x1, other arithmetic: none -> 1.96 us  [body(): return (4.0 * (own + other.astype(f32))).reshape(mine, depth)]
    unnamed x1 -> x0, local copies, waits for them, and re-layouts: 1.87 us -> none
where the time goes in v3:
time: 95.3 us; the launch traced here: 95.2 us
  Pallas kernels  93.3 us (98%)
  other arithmetic  1.96 us (2%)
    pallas_call x1, Pallas kernels, body(): pl.pallas_call(kernel, out_shape=(jax.ShapeDtypeStruct((K, mine // K, dep...  93.3 us
    reshape x1, other arithmetic, body(): return (4.0 * (own + other.astype(f32))).reshape(mine, depth)  1.96 us

profile of v3, /device:TPU:0, one launch (start us, length us, event | category | flops | bytes accessed | tf_op | source)
XLA Modules:
  0.0 95.2 jit_solution(10769938913358001492)
XLA Ops:
  0.0 93.3 %shard_map.37 = (f32[4,8,4096]{2,1,0:T(8,128)}, bf16[4,8,4096]{2,1,0:T(8,128)(2,1)}) custom-call(bf16[1024,4096]{1,0:T(8,128)(2,1)} %feat_hbm.1, bf16[32,4096]{1,0:T(8,128)(2,1)} %w_hbm.1, bf16[32,4096]{1,0:T(8,128)(2,1)} %d_hbm.1), custom_call_target="tpu_custom_call" | custom-call | tf_op jit(solution)/shard_map/pallas_call | solution.py:302
  93.3 2.0 %multiply_bitcast_fusion = f32[32,4096]{1,0:T(8,128)} fusion(f32[4,8,4096]{2,1,0:T(8,128)} %get-tuple-element.7, bf16[4,8,4096]{2,1,0:T(8,128)(2,1)} %get-tuple-element.8), kind=kLoop, calls=%fused_computation | loop fusion | flops 393216 | bytes 1310720 | tf_op jit(solution)/shard_map/reshape | solution.py:338

commit v4 on v3

--- a/solution.py
+++ b/solution.py
@@ -11,37 +11,39 @@
 BY_PIECE = {0: 0, 1: 1, 3: 1, 2: 2, 4: 2, 5: 3, 6: 4, 13: 5, 14: 6, 15: 7, 16: 7, 17: 8}
 BY_PIECE |= {25: 9, 26: 10, 28: 10, 29: 10, 31: 11}
 BY_CHUNK = {7: 0, 8: 0, 9: 0, 10: 0, 11: 0, 12: 0, 18: 1, 21: 1, 22: 1, 23: 1, 19: 2, 20: 3, 24: 4}
-SENDS = 64
+BY_CHUNK |= {32: 5}
+SENDS = 56
 PAIRED = (2, 3)
+PAIR_FIRST = (3, 1)
 NAMES = (
     "gather_start", "gather_second", "gather_forward", "gather_last",
     "scores", "scores_far", "scores_second", "scores_pair", "curvature", "", "",
-    "terms", "terms_first", "", "terms_pair",
+    "terms", "terms_first", "terms_second", "terms_pair",
 )
 ORDER = (
-    (0, 0, 0, 0), (0, 0, 1, 0), (0, 1, 0, 0), (1, 0, 0, 0), (1, 0, 1, 0), (1, 1, 0, 4),
-    (2, 0, 0, 4), (2, 0, 1, 4), (0, 1, 1, 0), (2, 1, 0, 3), (3, 0, 0, 3), (1, 1, 1, 3),
-    (0, 2, 0, 0), (3, 0, 1, 3), (4, 0, 0, 1), (4, 0, 1, 0), (2, 1, 1, 8), (3, 1, 0, 0),
-    (0, 2, 1, 0), (6, 0, 0, 6), (1, 2, 0, 0), (6, 0, 1, 4), (3, 1, 1, 1), (1, 2, 1, 6),
-    (4, 1, 0, 0), (2, 2, 0, 3), (7, 0, 0, 0), (4, 1, 1, 0), (2, 2, 1, 0), (0, 3, 0, 0),
-    (0, 3, 1, 0), (8, 0, 0, 14), (7, 0, 1, 0), (3, 2, 0, 0), (6, 1, 0, 0), (3, 2, 1, 5),
-    (1, 3, 0, 2), (4, 2, 0, 5), (1, 3, 1, 0), (6, 1, 1, 0), (4, 2, 1, 0), (2, 3, 0, 7),
-    (5, 2, 0, 16), (8, 0, 1, 0), (2, 3, 1, 0), (5, 2, 1, 3), (3, 3, 0, 6), (7, 1, 1, 5),
-    (6, 2, 0, 0), (7, 1, 0, 0), (3, 3, 1, 0), (4, 3, 0, 7), (6, 2, 1, 0), (8, 1, 0, 13),
-    (4, 3, 1, 0), (5, 3, 0, 5), (7, 2, 0, 0), (8, 1, 1, 0), (11, 0, 0, 0), (11, 0, 1, 0),
-    (5, 3, 1, 6), (6, 3, 0, 3), (12, 0, 0, 0), (7, 2, 1, 0), (6, 3, 1, 5), (8, 2, 0, 0),
-    (11, 1, 0, 9), (8, 2, 1, 0), (11, 1, 1, 0), (12, 0, 1, 0), (12, 1, 0, 7), (7, 3, 0, 0),
-    (7, 3, 1, 6), (12, 1, 1, 0), (8, 3, 1, 0), (11, 2, 0, 6), (8, 3, 0, 0), (11, 2, 1, 0),
-    (14, 1, 0, 0), (14, 0, 0, 0), (14, 0, 1, 0), (12, 2, 0, 17), (12, 2, 1, 3), (11, 3, 0, 1),
-    (14, 1, 1, 0), (12, 3, 0, 19), (11, 3, 1, 0), (12, 3, 1, 5), (14, 2, 1, 0), (14, 2, 0, 0),
-    (14, 3, 0, 5), (14, 3, 1, 1),
+    (0, 0, 0, 0), (0, 0, 1, 0), (0, 1, 1, 0), (1, 0, 0, 0), (1, 0, 1, 0), (1, 1, 1, 4),
+    (2, 0, 0, 4), (2, 0, 1, 4), (0, 1, 0, 0), (3, 0, 0, 3), (1, 1, 0, 6), (0, 2, 1, 0),
+    (3, 0, 1, 4), (2, 1, 1, 0), (4, 0, 0, 0), (2, 1, 0, 10), (4, 0, 1, 0), (1, 2, 1, 0),
+    (0, 2, 0, 0), (6, 0, 0, 4), (1, 2, 0, 5), (3, 1, 1, 0), (0, 3, 0, 0), (6, 0, 1, 0),
+    (3, 1, 0, 0), (2, 2, 1, 10), (4, 1, 0, 2), (7, 0, 0, 4), (2, 2, 0, 3), (1, 3, 0, 0),
+    (0, 3, 1, 0), (4, 1, 1, 0), (8, 0, 0, 8), (3, 2, 1, 0), (7, 0, 1, 0), (3, 2, 0, 3),
+    (6, 1, 0, 0), (1, 3, 1, 0), (4, 2, 0, 11), (6, 1, 1, 0), (2, 3, 0, 0), (4, 2, 1, 0),
+    (2, 3, 1, 11), (7, 1, 0, 14), (5, 2, 0, 0), (8, 0, 1, 0), (5, 2, 1, 0), (3, 3, 0, 0),
+    (3, 3, 1, 6), (7, 1, 1, 0), (8, 1, 0, 0), (6, 2, 0, 0), (4, 3, 0, 0), (4, 3, 1, 0),
+    (8, 1, 1, 0), (11, 0, 0, 0), (5, 3, 0, 28), (6, 2, 1, 0), (7, 2, 0, 7), (11, 0, 1, 0),
+    (12, 0, 0, 0), (5, 3, 1, 0), (11, 1, 0, 3), (6, 3, 0, 0), (11, 1, 1, 0), (12, 1, 0, 11),
+    (7, 2, 1, 0), (6, 3, 1, 0), (12, 0, 1, 0), (8, 2, 0, 0), (7, 3, 0, 5), (12, 1, 1, 0),
+    (8, 2, 1, 0), (7, 3, 1, 5), (14, 1, 0, 0), (8, 3, 0, 0), (8, 3, 1, 7), (11, 2, 0, 0),
+    (11, 2, 1, 0), (12, 2, 0, 25), (14, 0, 0, 0), (14, 0, 1, 0), (12, 2, 1, 6), (14, 1, 1, 0),
+    (11, 3, 0, 0), (11, 3, 1, 0), (12, 3, 1, 10), (12, 3, 0, 0), (14, 2, 1, 1), (14, 2, 0, 0),
+    (13, 3, 1, 5), (14, 3, 0, 5), (14, 3, 1, 3),
 )
 
 
 def kernel(
     feat_hbm, w_hbm, d_hbm, mine_hbm, theirs_hbm,
     feat, w_ref, d_ref, gath, part, rf, r1, r2, r3, curv, hess, r4,
-    zs, zr, ys, out,
+    zs, zr, ys, out, ps, pr, qs, qr,
     load, store, send, by_piece, by_chunk, last,
 ):
     f32, bf16 = jnp.float32, jnp.bfloat16
@@ -81,6 +83,7 @@
     rows, depth = feat.shape
     wide, long = depth // PIECES, rows // PIECES
     slots, flying, waiting = list(range(SENDS)), [], [loads[2]]
+    unpacked = list(range(1, CHUNKS))
 
     def lanes(p):
         return pl.ds(p * wide, wide)
@@ -91,7 +94,7 @@
     def receive(k, p, number):
         if number in BY_PIECE:
             return by_piece.at[k, p, BY_PIECE[number]]
-        return by_chunk.at[k, BY_CHUNK[number]] if number in BY_CHUNK else last.at[0]
+        return by_chunk.at[k, BY_CHUNK[number]] if number in BY_CHUNK else last.at[k]
 
     def retire():
         slot, one = flying.pop(0)
@@ -137,7 +140,8 @@
         gath[k, z, yh, core] = both.astype(bf16)
 
     def gather_start(k, p):
-        if p == 0 and k > 0:
+        if k in unpacked:
+            unpacked.remove(k)
             pack(k)
         mine = gath.at[k, z, yh, core, :, lanes(p)]
         same(k, p, 0, mine, to_yh)
@@ -256,14 +260,42 @@
         both = hess[k, place, :, core, :, here] + r4[k, place, :, :, here]
         return both.reshape(16, wide)
 
+    def part_of(k, p, place, half):
+        return hess[k, place, half, core, :, lanes(p)] + r4[k, place, half, :, lanes(p)]
+
     def terms_first(k, p):
         arrived(k, p, 25, r4.at[k, :, :, :, lanes(p)])
+        if (k, p) == PAIR_FIRST:
+            for place in range(ZS):
+                ps[place] = part_of(k, p, place, 1 - yh).astype(bf16)
+            push(k, p, 32, ps, pr, to_yh)
+            return
         there = ((26, z_far, to_z_far), (28, z_up, to_z_up), (29, z_down, to_z_down))
         for slot, (number, place, device) in enumerate(there):
             zs[k, p, slot] = chip(k, p, place).astype(bf16)
             push(k, p, number, zs.at[k, p, slot], zr.at[k, p, slot], device)
 
+    def terms_second(k, p):
+        arrived(k, p, 32, pr)
+        there = (
+            (30, z_far, to_z_far, theirs_hbm.at[k, :, lanes(p)]),
+            (28, z_up, to_z_up, qr.at[0]),
+            (29, z_down, to_z_down, qr.at[1]),
+        )
+        for slot, (number, place, device, dst) in enumerate(there):
+            qs[slot] = (part_of(k, p, place, yh) + pr[place].astype(f32)).astype(bf16)
+            push(k, p, number, qs.at[slot], dst, device)
+
+    def keep(k, p, value):
+        out[k, p] = value
+        pltpu.make_async_copy(out.at[k, p], mine_hbm.at[k, :, lanes(p)], store.at[0]).start()
+
     def terms_pair(k, p):
+        if (k, p) == PAIR_FIRST:
+            arrived(k, p, 28, qr)
+            own = part_of(k, p, z, yh) + pr[z].astype(f32)
+            keep(k, p, own + qr[0].astype(f32) + qr[1].astype(f32))
+            return
         arrived(k, p, 26, zr.at[k, p])
         own = chip(k, p, z)
         for slot in range(3):
@@ -271,12 +303,11 @@
         first = yh == 0
         ys[k, p] = jnp.where(first, own[8:], own[:8]).astype(bf16)
         push(k, p, 30, ys.at[k, p], theirs_hbm.at[k, :, lanes(p)], to_yh)
-        out[k, p] = jnp.where(first, own[:8], own[8:])
-        pltpu.make_async_copy(out.at[k, p], mine_hbm.at[k, :, lanes(p)], store.at[0]).start()
+        keep(k, p, jnp.where(first, own[:8], own[8:]))
 
     steps = {one.__name__: one for one in (
         gather_start, gather_second, gather_forward, gather_last, scores, scores_far,
-        scores_second, scores_pair, curvature, terms, terms_first, terms_pair,
+        scores_second, scores_pair, curvature, terms, terms_first, terms_second, terms_pair,
     )}
     loads[0].wait()
     loads[1].wait()
@@ -286,7 +317,8 @@
         for _ in range(min(enough, len(flying))):
             retire()
         steps[NAMES[place]](k, p)
-    arrived(0, 0, 30, theirs_hbm)
+    for k in range(CHUNKS):
+        arrived(k, 0, 30, theirs_hbm.at[k])
     pltpu.make_async_copy(mine_hbm, mine_hbm, store.at[0]).wait()
     while flying:
         retire()
@@ -324,12 +356,16 @@
             vmem((K, Q, 3, 16, wide), bf16),
             vmem((K, Q, 8, wide), bf16),
             vmem((K, Q, 8, wide), f32),
+            vmem((ZS, 8, wide), bf16),
+            vmem((ZS, 8, wide), bf16),
+            vmem((3, 8, wide), bf16),
+            vmem((2, 8, wide), bf16),
             pltpu.SemaphoreType.DMA((3,)),
             pltpu.SemaphoreType.DMA((1,)),
             pltpu.SemaphoreType.DMA((SENDS,)),
             pltpu.SemaphoreType.DMA((K, Q, 12)),
-            pltpu.SemaphoreType.DMA((K, 5)),
-            pltpu.SemaphoreType.DMA((1,)),
+            pltpu.SemaphoreType.DMA((K, 6)),
+            pltpu.SemaphoreType.DMA((K,)),
         ],
         compiler_params=pltpu.CompilerParams(
             collective_id=0, has_side_effects=True, vmem_limit_bytes=62 * 2**20

time: 95.3 us -> 95.6 us (level)
  no operation moved by 1% of the time
where the time goes in v4:
time: 95.6 us; the launch traced here: 95.4 us
  Pallas kernels  93.5 us (98%)
  other arithmetic  1.96 us (2%)
    pallas_call x1, Pallas kernels, body(): pl.pallas_call(kernel, out_shape=(jax.ShapeDtypeStruct((K, mine // K, dep...  93.5 us
    reshape x1, other arithmetic, body(): return (4.0 * (own + other.astype(f32))).reshape(mine, depth)  1.96 us

profile of v4, /device:TPU:0, one launch (start us, length us, event | category | flops | bytes accessed | tf_op | source)
XLA Modules:
  0.0 95.4 jit_solution(358622300550283168)
XLA Ops:
  0.0 93.5 %shard_map.37 = (f32[4,8,4096]{2,1,0:T(8,128)}, bf16[4,8,4096]{2,1,0:T(8,128)(2,1)}) custom-call(bf16[1024,4096]{1,0:T(8,128)(2,1)} %feat_hbm.1, bf16[32,4096]{1,0:T(8,128)(2,1)} %w_hbm.1, bf16[32,4096]{1,0:T(8,128)(2,1)} %d_hbm.1), custom_call_target="tpu_custom_call" | custom-call | tf_op jit(solution)/shard_map/pallas_call | solution.py:334
  93.5 2.0 %multiply_bitcast_fusion = f32[32,4096]{1,0:T(8,128)} fusion(f32[4,8,4096]{2,1,0:T(8,128)} %get-tuple-element.7, bf16[4,8,4096]{2,1,0:T(8,128)(2,1)} %get-tuple-element.8), kind=kLoop, calls=%fused_computation | loop fusion | flops 393216 | bytes 1310720 | tf_op jit(solution)/shard_map/reshape | solution.py:374

commit v5 on v4

--- a/solution.py
+++ b/solution.py
@@ -15,28 +15,29 @@
 SENDS = 56
 PAIRED = (2, 3)
 PAIR_FIRST = (3, 1)
+RING_FIRST = (0, 1)
 NAMES = (
     "gather_start", "gather_second", "gather_forward", "gather_last",
     "scores", "scores_far", "scores_second", "scores_pair", "curvature", "", "",
     "terms", "terms_first", "terms_second", "terms_pair",
 )
 ORDER = (
-    (0, 0, 0, 0), (0, 0, 1, 0), (0, 1, 1, 0), (1, 0, 0, 0), (1, 0, 1, 0), (1, 1, 1, 4),
-    (2, 0, 0, 4), (2, 0, 1, 4), (0, 1, 0, 0), (3, 0, 0, 3), (1, 1, 0, 6), (0, 2, 1, 0),
-    (3, 0, 1, 4), (2, 1, 1, 0), (4, 0, 0, 0), (2, 1, 0, 10), (4, 0, 1, 0), (1, 2, 1, 0),
-    (0, 2, 0, 0), (6, 0, 0, 4), (1, 2, 0, 5), (3, 1, 1, 0), (0, 3, 0, 0), (6, 0, 1, 0),
-    (3, 1, 0, 0), (2, 2, 1, 10), (4, 1, 0, 2), (7, 0, 0, 4), (2, 2, 0, 3), (1, 3, 0, 0),
-    (0, 3, 1, 0), (4, 1, 1, 0), (8, 0, 0, 8), (3, 2, 1, 0), (7, 0, 1, 0), (3, 2, 0, 3),
-    (6, 1, 0, 0), (1, 3, 1, 0), (4, 2, 0, 11), (6, 1, 1, 0), (2, 3, 0, 0), (4, 2, 1, 0),
-    (2, 3, 1, 11), (7, 1, 0, 14), (5, 2, 0, 0), (8, 0, 1, 0), (5, 2, 1, 0), (3, 3, 0, 0),
-    (3, 3, 1, 6), (7, 1, 1, 0), (8, 1, 0, 0), (6, 2, 0, 0), (4, 3, 0, 0), (4, 3, 1, 0),
-    (8, 1, 1, 0), (11, 0, 0, 0), (5, 3, 0, 28), (6, 2, 1, 0), (7, 2, 0, 7), (11, 0, 1, 0),
-    (12, 0, 0, 0), (5, 3, 1, 0), (11, 1, 0, 3), (6, 3, 0, 0), (11, 1, 1, 0), (12, 1, 0, 11),
-    (7, 2, 1, 0), (6, 3, 1, 0), (12, 0, 1, 0), (8, 2, 0, 0), (7, 3, 0, 5), (12, 1, 1, 0),
-    (8, 2, 1, 0), (7, 3, 1, 5), (14, 1, 0, 0), (8, 3, 0, 0), (8, 3, 1, 7), (11, 2, 0, 0),
-    (11, 2, 1, 0), (12, 2, 0, 25), (14, 0, 0, 0), (14, 0, 1, 0), (12, 2, 1, 6), (14, 1, 1, 0),
-    (11, 3, 0, 0), (11, 3, 1, 0), (12, 3, 1, 10), (12, 3, 0, 0), (14, 2, 1, 1), (14, 2, 0, 0),
-    (13, 3, 1, 5), (14, 3, 0, 5), (14, 3, 1, 3),
+    (0, 0, 1, 0), (0, 0, 0, 0), (0, 1, 0, 0), (1, 0, 1, 0), (1, 0, 0, 0), (0, 1, 1, 0),
+    (1, 1, 0, 4), (2, 0, 1, 4), (2, 0, 0, 4), (0, 2, 0, 0), (1, 1, 1, 4), (3, 0, 1, 7),
+    (3, 0, 0, 5), (0, 2, 1, 0), (2, 1, 0, 0), (1, 2, 0, 2), (4, 0, 0, 4), (4, 0, 1, 0),
+    (2, 1, 1, 0), (1, 2, 1, 0), (6, 0, 0, 11), (0, 3, 0, 0), (2, 2, 0, 4), (3, 1, 1, 4),
+    (3, 1, 0, 0), (6, 0, 1, 0), (2, 2, 1, 7), (0, 3, 1, 0), (1, 3, 0, 0), (4, 1, 0, 0),
+    (7, 0, 0, 0), (4, 1, 1, 0), (7, 0, 1, 13), (3, 2, 0, 0), (1, 3, 1, 0), (8, 0, 0, 8),
+    (3, 2, 1, 0), (6, 1, 0, 2), (4, 2, 0, 0), (2, 3, 0, 0), (4, 2, 1, 0), (6, 1, 1, 0),
+    (2, 3, 1, 0), (5, 2, 0, 19), (7, 1, 0, 12), (3, 3, 0, 0), (5, 2, 1, 0), (8, 0, 1, 0),
+    (3, 3, 1, 0), (8, 1, 0, 7), (6, 2, 1, 1), (7, 1, 1, 0), (4, 3, 0, 0), (6, 2, 0, 0),
+    (4, 3, 1, 0), (11, 0, 0, 0), (5, 3, 0, 29), (8, 1, 1, 0), (5, 3, 1, 0), (6, 3, 0, 1),
+    (12, 0, 0, 0), (7, 2, 1, 0), (7, 2, 0, 0), (11, 1, 0, 7), (6, 3, 1, 0), (11, 1, 1, 0),
+    (8, 2, 1, 0), (12, 1, 0, 11), (8, 2, 0, 0), (7, 3, 0, 0), (12, 1, 1, 0), (11, 0, 1, 0),
+    (7, 3, 1, 8), (12, 0, 1, 0), (8, 3, 0, 0), (8, 3, 1, 7), (11, 2, 0, 0), (11, 2, 1, 0),
+    (14, 0, 0, 0), (12, 2, 0, 19), (11, 3, 0, 0), (11, 3, 1, 0), (14, 0, 1, 0), (14, 1, 1, 0),
+    (12, 2, 1, 0), (12, 3, 1, 20), (14, 1, 0, 0), (14, 2, 0, 1), (12, 3, 0, 0), (13, 3, 1, 0),
+    (14, 2, 1, 0), (14, 3, 0, 9), (14, 3, 1, 2),
 )
 
 
@@ -144,12 +145,40 @@
             unpacked.remove(k)
             pack(k)
         mine = gath.at[k, z, yh, core, :, lanes(p)]
-        same(k, p, 0, mine, to_yh)
         same(k, p, 1, mine, to_z_up)
         same(k, p, 2, mine, to_z_down)
+        same(k, p, 0, mine, to_yh)
         same(k, p, 7, mine, to_core)
 
+    def ring_second(k, p):
+        half = wide // 2
+        down = gath.at[k, z_down, yh, core]
+        arrived(k, p, 1, down.at[:, lanes(p)])
+        same(k, p, 5, down.at[:, pl.ds(p * wide, half)], to_z_up)
+        same(k, p, 0, down.at[:, lanes(p)], to_yh)
+        same(k, p, 9, down.at[:, lanes(p)], to_core)
+        up = gath.at[k, z_up, yh, core]
+        arrived(k, p, 2, up.at[:, lanes(p)])
+        same(k, p, 6, up.at[:, pl.ds(p * wide + half, half)], to_z_down)
+        same(k, p, 0, up.at[:, lanes(p)], to_yh)
+        same(k, p, 10, up.at[:, lanes(p)], to_core)
+
+    def ring_forward(k, p):
+        half = wide // 2
+        far = gath.at[k, z_far, yh, core]
+        arrived(k, p, 5, far.at[:, pl.ds(p * wide, half)])
+        arrived(k, p, 6, far.at[:, pl.ds(p * wide + half, half)])
+        same(k, p, 0, far.at[:, lanes(p)], to_yh)
+        same(k, p, 11, far.at[:, lanes(p)], to_core)
+
+    def ring_last(k, p):
+        theirs = gath.at[k, :, 1 - yh, core, :, lanes(p)]
+        arrived(k, p, 0, theirs)
+        same(k, p, 12, theirs, to_core)
+
     def gather_second(k, p):
+        if (k, p) == RING_FIRST:
+            return ring_second(k, p)
         theirs = gath.at[k, z, 1 - yh, core, :, lanes(p)]
         arrived(k, p, 0, theirs)
         same(k, p, 3, theirs, to_z_up)
@@ -157,6 +186,8 @@
         same(k, p, 8, theirs, to_core)
 
     def gather_forward(k, p):
+        if (k, p) == RING_FIRST:
+            return ring_forward(k, p)
         arrived(k, p, 1, gath.at[k, z_down, :, core, :, lanes(p)])
         same(k, p, 5, gath.at[k, z_down, 0, core, :, lanes(p)], to_z_up)
         arrived(k, p, 2, gath.at[k, z_up, :, core, :, lanes(p)])
@@ -165,6 +196,8 @@
         same(k, p, 10, gath.at[k, z_up, :, core, :, lanes(p)], to_core)
 
     def gather_last(k, p):
+        if (k, p) == RING_FIRST:
+            return ring_last(k, p)
         arrived(k, p, 5, gath.at[k, z_far, 0, core, :, lanes(p)])
         same(k, p, 11, gath.at[k, z_far, 0, core, :, lanes(p)], to_core)
         arrived(k, p, 6, gath.at[k, z_far, 1, core, :, lanes(p)])

time: 95.6 us -> 92.8 us (0.971); the launches traced: 95.4 us -> 91.3 us
  Pallas kernels: 93.5 us -> 89.4 us
    pallas_call x1, Pallas kernels: 93.5 us -> 89.4 us  [body(): pl.pallas_call(kernel, out_shape=(jax.ShapeDtypeStruct((K, mine // K, dep...]
where the time goes in v5:
time: 92.8 us; the launch traced here: 91.3 us
  Pallas kernels  89.4 us (96%)
  other arithmetic  1.96 us (2%)
    pallas_call x1, Pallas kernels, body(): pl.pallas_call(kernel, out_shape=(jax.ShapeDtypeStruct((K, mine // K, dep...  89.4 us
    reshape x1, other arithmetic, body(): return (4.0 * (own + other.astype(f32))).reshape(mine, depth)  1.96 us

profile of v5, /device:TPU:0, one launch (start us, length us, event | category | flops | bytes accessed | tf_op | source)
XLA Modules:
  0.0 91.3 jit_solution(8070029032871024580)
XLA Ops:
  0.0 89.4 %shard_map.37 = (f32[4,8,4096]{2,1,0:T(8,128)}, bf16[4,8,4096]{2,1,0:T(8,128)(2,1)}) custom-call(bf16[1024,4096]{1,0:T(8,128)(2,1)} %feat_hbm.1, bf16[32,4096]{1,0:T(8,128)(2,1)} %w_hbm.1, bf16[32,4096]{1,0:T(8,128)(2,1)} %d_hbm.1), custom_call_target="tpu_custom_call" | custom-call | tf_op jit(solution)/shard_map/pallas_call | solution.py:367
  89.4 2.0 %multiply_bitcast_fusion = f32[32,4096]{1,0:T(8,128)} fusion(f32[4,8,4096]{2,1,0:T(8,128)} %get-tuple-element.7, bf16[4,8,4096]{2,1,0:T(8,128)(2,1)} %get-tuple-element.8), kind=kLoop, calls=%fused_computation | loop fusion | flops 393216 | bytes 1310720 | tf_op jit(solution)/shard_map/reshape | solution.py:407

commit v6 on v5

--- a/solution.py
+++ b/solution.py
@@ -12,7 +12,7 @@
 BY_PIECE |= {25: 9, 26: 10, 28: 10, 29: 10, 31: 11}
 BY_CHUNK = {7: 0, 8: 0, 9: 0, 10: 0, 11: 0, 12: 0, 18: 1, 21: 1, 22: 1, 23: 1, 19: 2, 20: 3, 24: 4}
 BY_CHUNK |= {32: 5}
-SENDS = 56
+SENDS = 48
 PAIRED = (2, 3)
 PAIR_FIRST = (3, 1)
 RING_FIRST = (0, 1)
@@ -22,22 +22,22 @@
     "terms", "terms_first", "terms_second", "terms_pair",
 )
 ORDER = (
-    (0, 0, 1, 0), (0, 0, 0, 0), (0, 1, 0, 0), (1, 0, 1, 0), (1, 0, 0, 0), (0, 1, 1, 0),
-    (1, 1, 0, 4), (2, 0, 1, 4), (2, 0, 0, 4), (0, 2, 0, 0), (1, 1, 1, 4), (3, 0, 1, 7),
-    (3, 0, 0, 5), (0, 2, 1, 0), (2, 1, 0, 0), (1, 2, 0, 2), (4, 0, 0, 4), (4, 0, 1, 0),
-    (2, 1, 1, 0), (1, 2, 1, 0), (6, 0, 0, 11), (0, 3, 0, 0), (2, 2, 0, 4), (3, 1, 1, 4),
-    (3, 1, 0, 0), (6, 0, 1, 0), (2, 2, 1, 7), (0, 3, 1, 0), (1, 3, 0, 0), (4, 1, 0, 0),
-    (7, 0, 0, 0), (4, 1, 1, 0), (7, 0, 1, 13), (3, 2, 0, 0), (1, 3, 1, 0), (8, 0, 0, 8),
-    (3, 2, 1, 0), (6, 1, 0, 2), (4, 2, 0, 0), (2, 3, 0, 0), (4, 2, 1, 0), (6, 1, 1, 0),
-    (2, 3, 1, 0), (5, 2, 0, 19), (7, 1, 0, 12), (3, 3, 0, 0), (5, 2, 1, 0), (8, 0, 1, 0),
-    (3, 3, 1, 0), (8, 1, 0, 7), (6, 2, 1, 1), (7, 1, 1, 0), (4, 3, 0, 0), (6, 2, 0, 0),
-    (4, 3, 1, 0), (11, 0, 0, 0), (5, 3, 0, 29), (8, 1, 1, 0), (5, 3, 1, 0), (6, 3, 0, 1),
-    (12, 0, 0, 0), (7, 2, 1, 0), (7, 2, 0, 0), (11, 1, 0, 7), (6, 3, 1, 0), (11, 1, 1, 0),
-    (8, 2, 1, 0), (12, 1, 0, 11), (8, 2, 0, 0), (7, 3, 0, 0), (12, 1, 1, 0), (11, 0, 1, 0),
-    (7, 3, 1, 8), (12, 0, 1, 0), (8, 3, 0, 0), (8, 3, 1, 7), (11, 2, 0, 0), (11, 2, 1, 0),
-    (14, 0, 0, 0), (12, 2, 0, 19), (11, 3, 0, 0), (11, 3, 1, 0), (14, 0, 1, 0), (14, 1, 1, 0),
-    (12, 2, 1, 0), (12, 3, 1, 20), (14, 1, 0, 0), (14, 2, 0, 1), (12, 3, 0, 0), (13, 3, 1, 0),
-    (14, 2, 1, 0), (14, 3, 0, 9), (14, 3, 1, 2),
+    (0, 0, 1, 0), (0, 0, 0, 0), (0, 1, 1, 0), (1, 0, 1, 0), (1, 0, 0, 0), (0, 1, 0, 0),
+    (1, 1, 1, 4), (2, 0, 1, 4), (2, 0, 0, 4), (1, 1, 0, 4), (3, 0, 1, 7), (2, 1, 1, 0),
+    (3, 0, 0, 5), (0, 2, 1, 0), (4, 0, 0, 2), (2, 1, 0, 0), (0, 2, 0, 0), (4, 0, 1, 0),
+    (1, 2, 1, 0), (3, 1, 1, 0), (1, 2, 0, 15), (6, 0, 0, 0), (3, 1, 0, 0), (0, 3, 0, 0),
+    (4, 1, 0, 4), (2, 2, 1, 3), (4, 1, 1, 0), (2, 2, 0, 0), (6, 0, 1, 0), (0, 3, 1, 0),
+    (3, 2, 1, 14), (1, 3, 0, 0), (7, 0, 0, 0), (6, 1, 0, 0), (6, 1, 1, 10), (3, 2, 0, 7),
+    (1, 3, 1, 0), (4, 2, 0, 2), (2, 3, 0, 4), (7, 0, 1, 0), (4, 2, 1, 0), (2, 3, 1, 0),
+    (5, 2, 0, 12), (8, 0, 0, 0), (3, 3, 0, 1), (8, 0, 1, 1), (5, 2, 1, 0), (3, 3, 1, 0),
+    (6, 2, 0, 0), (7, 1, 0, 0), (4, 3, 0, 13), (4, 3, 1, 0), (6, 2, 1, 0), (7, 1, 1, 0),
+    (11, 0, 0, 0), (5, 3, 0, 25), (8, 1, 0, 0), (12, 0, 0, 2), (5, 3, 1, 0), (8, 1, 1, 0),
+    (11, 0, 1, 0), (6, 3, 0, 5), (7, 2, 1, 0), (12, 0, 1, 4), (7, 2, 0, 0), (6, 3, 1, 5),
+    (8, 2, 1, 5), (11, 1, 0, 0), (11, 1, 1, 0), (8, 2, 0, 0), (12, 1, 1, 12), (7, 3, 0, 0),
+    (7, 3, 1, 7), (12, 1, 0, 0), (8, 3, 0, 0), (8, 3, 1, 5), (11, 2, 0, 0), (14, 1, 1, 0),
+    (11, 2, 1, 0), (12, 2, 0, 19), (14, 0, 1, 0), (11, 3, 0, 0), (11, 3, 1, 0), (12, 2, 1, 0),
+    (14, 1, 0, 0), (12, 3, 1, 18), (14, 0, 0, 0), (12, 3, 0, 0), (14, 2, 1, 0), (14, 2, 0, 0),
+    (13, 3, 1, 6), (14, 3, 0, 3), (14, 3, 1, 3),
 )
 
 
@@ -76,7 +76,7 @@
     barrier = pltpu.get_barrier_semaphore()
     partners = [
         to_core, to_yl, to_z_up, to_z_down, to_x_up, to_x_down,
-        to_yh, to_z_far, to_x_far, *across,
+        to_yh,
     ]
     for partner in partners:
         pl.semaphore_signal(barrier, inc=1, device_id=partner, device_id_type=mesh_ids)

time: 92.8 us -> 92 us (level)
  no operation moved by 1% of the time
where the time goes in v6:
time: 92 us; the launch traced here: 91.2 us
  Pallas kernels  89.2 us (97%)
  other arithmetic  1.96 us (2%)
    pallas_call x1, Pallas kernels, body(): pl.pallas_call(kernel, out_shape=(jax.ShapeDtypeStruct((K, mine // K, dep...  89.2 us
    reshape x1, other arithmetic, body(): return (4.0 * (own + other.astype(f32))).reshape(mine, depth)  1.96 us

profile of v6, /device:TPU:0, one launch (start us, length us, event | category | flops | bytes accessed | tf_op | source)
XLA Modules:
  0.0 91.2 jit_solution(9930089514501818315)
XLA Ops:
  0.0 89.2 %shard_map.37 = (f32[4,8,4096]{2,1,0:T(8,128)}, bf16[4,8,4096]{2,1,0:T(8,128)(2,1)}) custom-call(bf16[1024,4096]{1,0:T(8,128)(2,1)} %feat_hbm.1, bf16[32,4096]{1,0:T(8,128)(2,1)} %w_hbm.1, bf16[32,4096]{1,0:T(8,128)(2,1)} %d_hbm.1), custom_call_target="tpu_custom_call" | custom-call | tf_op jit(solution)/shard_map/pallas_call | solution.py:367
  89.2 2.0 %multiply_bitcast_fusion = f32[32,4096]{1,0:T(8,128)} fusion(f32[4,8,4096]{2,1,0:T(8,128)} %get-tuple-element.7, bf16[4,8,4096]{2,1,0:T(8,128)(2,1)} %get-tuple-element.8), kind=kLoop, calls=%fused_computation | loop fusion | flops 393216 | bytes 1310720 | tf_op jit(solution)/shard_map/reshape | solution.py:407

commit v7 on v6

--- a/solution.py
+++ b/solution.py
@@ -13,7 +13,7 @@
 BY_CHUNK = {7: 0, 8: 0, 9: 0, 10: 0, 11: 0, 12: 0, 18: 1, 21: 1, 22: 1, 23: 1, 19: 2, 20: 3, 24: 4}
 BY_CHUNK |= {32: 5}
 SENDS = 48
-PAIRED = (2, 3)
+PAIRED = (1, 2, 3)
 PAIR_FIRST = (3, 1)
 RING_FIRST = (0, 1)
 NAMES = (
@@ -22,22 +22,22 @@
     "terms", "terms_first", "terms_second", "terms_pair",
 )
 ORDER = (
-    (0, 0, 1, 0), (0, 0, 0, 0), (0, 1, 1, 0), (1, 0, 1, 0), (1, 0, 0, 0), (0, 1, 0, 0),
-    (1, 1, 1, 4), (2, 0, 1, 4), (2, 0, 0, 4), (1, 1, 0, 4), (3, 0, 1, 7), (2, 1, 1, 0),
-    (3, 0, 0, 5), (0, 2, 1, 0), (4, 0, 0, 2), (2, 1, 0, 0), (0, 2, 0, 0), (4, 0, 1, 0),
-    (1, 2, 1, 0), (3, 1, 1, 0), (1, 2, 0, 15), (6, 0, 0, 0), (3, 1, 0, 0), (0, 3, 0, 0),
-    (4, 1, 0, 4), (2, 2, 1, 3), (4, 1, 1, 0), (2, 2, 0, 0), (6, 0, 1, 0), (0, 3, 1, 0),
-    (3, 2, 1, 14), (1, 3, 0, 0), (7, 0, 0, 0), (6, 1, 0, 0), (6, 1, 1, 10), (3, 2, 0, 7),
-    (1, 3, 1, 0), (4, 2, 0, 2), (2, 3, 0, 4), (7, 0, 1, 0), (4, 2, 1, 0), (2, 3, 1, 0),
-    (5, 2, 0, 12), (8, 0, 0, 0), (3, 3, 0, 1), (8, 0, 1, 1), (5, 2, 1, 0), (3, 3, 1, 0),
-    (6, 2, 0, 0), (7, 1, 0, 0), (4, 3, 0, 13), (4, 3, 1, 0), (6, 2, 1, 0), (7, 1, 1, 0),
-    (11, 0, 0, 0), (5, 3, 0, 25), (8, 1, 0, 0), (12, 0, 0, 2), (5, 3, 1, 0), (8, 1, 1, 0),
-    (11, 0, 1, 0), (6, 3, 0, 5), (7, 2, 1, 0), (12, 0, 1, 4), (7, 2, 0, 0), (6, 3, 1, 5),
-    (8, 2, 1, 5), (11, 1, 0, 0), (11, 1, 1, 0), (8, 2, 0, 0), (12, 1, 1, 12), (7, 3, 0, 0),
-    (7, 3, 1, 7), (12, 1, 0, 0), (8, 3, 0, 0), (8, 3, 1, 5), (11, 2, 0, 0), (14, 1, 1, 0),
-    (11, 2, 1, 0), (12, 2, 0, 19), (14, 0, 1, 0), (11, 3, 0, 0), (11, 3, 1, 0), (12, 2, 1, 0),
-    (14, 1, 0, 0), (12, 3, 1, 18), (14, 0, 0, 0), (12, 3, 0, 0), (14, 2, 1, 0), (14, 2, 0, 0),
-    (13, 3, 1, 6), (14, 3, 0, 3), (14, 3, 1, 3),
+    (0, 0, 0, 0), (0, 1, 1, 0), (0, 0, 1, 0), (0, 1, 0, 0), (1, 0, 0, 0), (1, 0, 1, 0),
+    (1, 1, 1, 0), (1, 1, 0, 8), (2, 0, 1, 4), (2, 0, 0, 0), (2, 1, 1, 7), (2, 1, 0, 4),
+    (0, 2, 1, 0), (0, 2, 0, 0), (3, 0, 1, 5), (3, 0, 0, 3), (4, 0, 0, 2), (3, 1, 0, 6),
+    (3, 1, 1, 0), (0, 3, 0, 0), (4, 0, 1, 0), (1, 2, 0, 0), (4, 1, 0, 0), (1, 2, 1, 0),
+    (6, 0, 0, 10), (4, 1, 1, 0), (2, 2, 0, 14), (5, 1, 0, 0), (6, 0, 1, 0), (2, 2, 1, 6),
+    (1, 3, 0, 0), (5, 1, 1, 0), (0, 3, 1, 0), (6, 1, 0, 4), (7, 0, 0, 0), (3, 2, 0, 1),
+    (3, 2, 1, 5), (1, 3, 1, 0), (7, 0, 1, 6), (6, 1, 1, 0), (4, 2, 0, 0), (2, 3, 0, 0),
+    (4, 2, 1, 0), (8, 0, 0, 0), (2, 3, 1, 0), (5, 2, 0, 15), (7, 1, 0, 0), (8, 0, 1, 0),
+    (3, 3, 0, 4), (5, 2, 1, 7), (3, 3, 1, 0), (7, 1, 1, 0), (6, 2, 0, 7), (4, 3, 0, 0),
+    (6, 2, 1, 14), (4, 3, 1, 0), (11, 0, 0, 0), (5, 3, 0, 14), (8, 1, 1, 0), (11, 0, 1, 0),
+    (5, 3, 1, 3), (8, 1, 0, 0), (12, 0, 0, 0), (7, 2, 0, 0), (6, 3, 0, 1), (7, 2, 1, 0),
+    (6, 3, 1, 4), (8, 2, 1, 10), (8, 2, 0, 0), (12, 0, 1, 0), (7, 3, 0, 13), (11, 1, 0, 0),
+    (11, 1, 1, 0), (7, 3, 1, 3), (12, 1, 0, 0), (8, 3, 0, 0), (12, 1, 1, 0), (8, 3, 1, 5),
+    (11, 2, 0, 0), (11, 2, 1, 0), (12, 2, 0, 19), (11, 3, 0, 9), (11, 3, 1, 0), (12, 2, 1, 0),
+    (14, 1, 0, 0), (12, 3, 1, 11), (12, 3, 0, 0), (14, 0, 1, 0), (14, 0, 0, 0), (14, 1, 1, 0),
+    (14, 2, 1, 2), (13, 3, 1, 5), (14, 2, 0, 0), (14, 3, 0, 2), (14, 3, 1, 0),
 )
 
 

time: 92 us -> 92.7 us (level)
  no operation moved by 1% of the time
where the time goes in v7:
time: 92.7 us; the launch traced here: 91.2 us
  Pallas kernels  89.3 us (96%)
  other arithmetic  1.96 us (2%)
    pallas_call x1, Pallas kernels, body(): pl.pallas_call(kernel, out_shape=(jax.ShapeDtypeStruct((K, mine // K, dep...  89.3 us
    reshape x1, other arithmetic, body(): return (4.0 * (own + other.astype(f32))).reshape(mine, depth)  1.96 us

profile of v7, /device:TPU:0, one launch (start us, length us, event | category | flops | bytes accessed | tf_op | source)
XLA Modules:
  0.0 91.2 jit_solution(17135371654484301009)
XLA Ops:
  0.0 89.3 %shard_map.37 = (f32[4,8,4096]{2,1,0:T(8,128)}, bf16[4,8,4096]{2,1,0:T(8,128)(2,1)}) custom-call(bf16[1024,4096]{1,0:T(8,128)(2,1)} %feat_hbm.1, bf16[32,4096]{1,0:T(8,128)(2,1)} %w_hbm.1, bf16[32,4096]{1,0:T(8,128)(2,1)} %d_hbm.1), custom_call_target="tpu_custom_call" | custom-call | tf_op jit(solution)/shard_map/pallas_call | solution.py:367
  89.3 2.0 %multiply_bitcast_fusion = f32[32,4096]{1,0:T(8,128)} fusion(f32[4,8,4096]{2,1,0:T(8,128)} %get-tuple-element.7, bf16[4,8,4096]{2,1,0:T(8,128)(2,1)} %get-tuple-element.8), kind=kLoop, calls=%fused_computation | loop fusion | flops 393216 | bytes 1310720 | tf_op jit(solution)/shard_map/reshape | solution.py:407
